TPU v7x, 128 devices: a whole 4x4x4 slice. The times are simulated.
128 devices in a mesh: seg: 32 (over y_lo, x, z), rep: 4 (over y_hi, core).
Axes of the slice: x: 4, y: 4 (y_hi: 2, y_lo: 2; y = y_hi * 2 + y_lo), z: 4, core: 2. Of those that a mesh axis runs over, the one named last changes fastest.
Arguments:
- decoder_rows: bfloat16 [256, 4096], P('rep', 'seg'), may hold values from -2000 to 2000
- norm_gain: float32 [4096], replicated, may hold values from 0.5 to 1.5
- query_weight: bfloat16 [4096, 4096], P('rep', 'seg'), may hold values from -1 to 1
- key_codes: bfloat16 [4, 16384, 4096], P('rep', 'seg'), may hold values from -127 to 127, as said below
- key_scale: float32 [4, 128, 64], P('rep', 'seg'), may hold values from 0.5 to 1.5
- value_codes: bfloat16 [4, 16384, 4096], P('rep', 'seg'), may hold values from -6 to 6
- value_scale: float32 [4, 128, 64], P('rep', 'seg'), may hold values from 0.5 to 2
- enc_lengths: int32 [4], P('rep'), may hold values from 4096 to 16384
- output_weight: bfloat16 [4096, 4096], P('seg', 'rep'), may hold values from -0.09375 to 0.09375
Outputs:
- update: bfloat16 [256, 4096], P('rep', 'seg')
Inputs may be any that keep to these rules, and one draw needn't show every extreme that they name: `key_codes`: codes of a block times its scale give the cached keys.
All inputs are finite; a program needn't handle non-finite values.
Results may differ from a plain program's by a relative error of at most 0.011.
Values may be sent and summed in bfloat16 or wider, within the bound.
No kernel may reach another device: no remote copies, remote signals or barrier semaphores. Data moves between devices by JAX's collectives and lax.ppermute only.
A program may use at most 64 MiB of HBM per device.

v0:
```python
import jax
import jax.numpy as jnp
from jax import lax
from jax.sharding import PartitionSpec as P


def laid_out(tiles, dim):
    tiles = jnp.moveaxis(tiles, 0, dim)
    dims = tiles.shape
    return tiles.reshape(*dims[:dim], dims[dim] * dims[dim + 1], *dims[dim + 2 :])


def from_everyone(shard, axis):
    count = lax.axis_size(axis)
    return lax.all_to_all(
        jnp.broadcast_to(shard[None], (count, *shard.shape)), axis, 0, 0, tiled=True
    )


def gathered_copies(shard, axis, dim):
    return laid_out(from_everyone(shard, axis), dim)


def side_by_side(arrays, axis, split_dim, concat_dim, along):
    ends, at = ([], 0)
    for a in arrays[:-1]:
        at += a.shape[along]
        ends.append(at)
    both = jnp.concatenate(arrays, axis=along)
    return tuple(
        jnp.split(
            lax.all_to_all(both, axis, split_axis=split_dim, concat_axis=concat_dim, tiled=True),
            ends,
            axis=along,
        )
    )


def in_blocks(shard, dim, count):
    before, after = (shard.shape[:dim], shard.shape[dim + 1 :])
    return jnp.moveaxis(shard.reshape(*before, count, -1, *after), dim, 0)


def sent_and_summed(shard, axis, dim):
    tiles = in_blocks(shard, dim, lax.axis_size(axis))
    arrived = lax.all_to_all(tiles, axis, split_axis=0, concat_axis=0, tiled=True)
    return arrived.sum(axis=0)


def per_device(
    decoder_rows,
    norm_gain,
    query_weight,
    key_codes,
    key_scale,
    value_codes,
    value_scale,
    enc_lengths,
    output_weight,
):
    gathered = gathered_copies(decoder_rows, "seg", 1)
    widened = gathered.astype(jnp.float32)
    variance = jnp.mean(widened * widened, axis=-1, keepdims=True)
    normed = (widened * lax.rsqrt(variance + 1e-06) * norm_gain[None, :]).astype(jnp.bfloat16)
    query_own = jnp.dot(
        normed, gathered_copies(query_weight, "rep", 0), preferred_element_type=jnp.float32
    ).astype(jnp.bfloat16)
    queries = gathered_copies(query_own, "seg", 1)
    docs_here, seg_length, inner_width = key_codes.shape
    head_count = key_scale.shape[2]
    head_dim = inner_width // head_count
    block_length = seg_length // key_scale.shape[1]
    per_doc = queries.shape[0] // docs_here
    row_count = docs_here * per_doc
    first_pos = lax.axis_index("seg") * seg_length
    positions = first_pos + jnp.arange(seg_length, dtype=jnp.int32)

    def one_doc(group_members):
        (
            document_query,
            document_keys,
            document_values,
            document_key_scale,
            document_value_scale,
            document_length,
        ) = group_members
        split_query = document_query.reshape(per_doc, head_count, head_dim)
        split_keys = document_keys.reshape(seg_length, head_count, head_dim)
        split_values = document_values.reshape(seg_length, head_count, head_dim)
        attention_scores = jnp.einsum(
            "qhd,khd->qhk", split_query, split_keys, preferred_element_type=jnp.float32
        )
        key_multiplier = jnp.repeat(document_key_scale, block_length, axis=0).T
        value_factor = jnp.repeat(document_value_scale, block_length, axis=0).T
        attention_scores = attention_scores * key_multiplier[None]
        usable = (positions < document_length)[None, None, :]
        attention_scores = jnp.where(usable, attention_scores, jnp.float32(-1e30))
        peaks = jnp.max(attention_scores, axis=-1)
        weights = jnp.where(usable, jnp.exp(attention_scores - peaks[..., None]), jnp.float32(0.0))
        totals = jnp.sum(weights, axis=-1)
        scaled = (weights * value_factor[None]).astype(jnp.bfloat16)
        attended = jnp.einsum(
            "qhk,khd->qhd", scaled, split_values, preferred_element_type=jnp.float32
        )
        return (peaks, totals, attended.reshape(per_doc, inner_width))

    query_docs = queries.reshape(docs_here, per_doc, inner_width)
    peaks, totals, outputs = lax.map(
        one_doc, (query_docs, key_codes, value_codes, key_scale, value_scale, enc_lengths)
    )
    peaks = peaks.reshape(row_count, head_count)
    totals = totals.reshape(row_count, head_count)
    outputs = outputs.reshape(row_count, inner_width)
    seg_count = lax.axis_size("seg")
    own_heads = head_count // seg_count
    received = (
        *side_by_side((peaks[None], totals[None]), "seg", 2, 0, 1),
        lax.all_to_all(outputs[None], "seg", split_axis=2, concat_axis=0, tiled=True),
    )
    peak_all, total_all, out_all = received
    largest = jnp.max(peak_all, axis=0)
    factor = jnp.exp(peak_all - largest[None])
    denominator = jnp.sum(factor * total_all, axis=0)
    numerator = jnp.sum(
        out_all.reshape(seg_count, row_count, own_heads, head_dim) * factor[..., None], axis=0
    )
    attn_own = (
        (numerator / denominator[..., None])
        .reshape(row_count, own_heads * head_dim)
        .astype(jnp.bfloat16)
    )
    partial_terms = jnp.dot(
        attn_own, gathered_copies(output_weight, "rep", 1), preferred_element_type=jnp.float32
    )
    return sent_and_summed(partial_terms, "seg", 1).astype(jnp.bfloat16)


def solution(mesh):
    placed = (
        P("rep", "seg"),
        P(),
        P("rep", "seg"),
        P("rep", "seg", None),
        P("rep", "seg", None),
        P("rep", "seg", None),
        P("rep", "seg", None),
        P("rep"),
        P("seg", "rep"),
    )
    return jax.shard_map(
        per_device, mesh=mesh, in_specs=placed, out_specs=P("rep", "seg"), check_vma=False
    )
```

profile of v0, /device:TPU:0, one launch (start us, length us, event | category | flops | bytes accessed | tf_op | source)
XLA Modules:
  0.0 186.5 jit_solution(13017367994925692182)
XLA Ops:
  0.0 0.0 copy-start.2
  0.0 0.0 copy-start.3
  0.0 0.9 broadcast_in_dim.84
  0.9 20.6 %all_to_all.58 = bf16[32,64,128]{2,1,0:T(8,128)(2,1)S(1)} all-to-all(bf16[32,64,128]{2,1,0:T(8,128)(2,1)S(1)} %broadcast_in_dim.84), channel_id=1, replica_groups=mesh['seg'=32,'rep'=4] {'seg'}, dimensions={0} | all-to-all | bytes 1048576 | tf_op jit(solution)/shard_map/all_to_all | solution.py:15
  21.5 2.1 %broadcast_in_dim.85 = bf16[4,1024,128]{2,1,0:T(8,128)(2,1)} broadcast(bf16[1024,128]{1,0:T(8,128)(2,1)} %param.11), dimensions={1,2} | broadcast | bytes 1310720 | tf_op jit(solution)/shard_map/broadcast_in_dim | solution.py:16
  23.5 4.2 %all-to-all-start.1 = ((bf16[4,1024,128]{2,1,0:T(8,128)(2,1)}), bf16[4,1024,128]{2,1,0:T(8,128)(2,1)S(1)}, u32[]{:S(2)}, u32[]{:S(2)}) async-start(bf16[4,1024,128]{2,1,0:T(8,128)(2,1)} %broadcast_in_dim.85), calls=%async_computation.1 | async-start | bytes 2097152 | tf_op jit(solution)/shard_map/all_to_all | solution.py:15
  27.7 0.2 fusion.13
  27.9 15.7 %all-to-all-done.1 = bf16[4,1024,128]{2,1,0:T(8,128)(2,1)S(1)} async-done(((bf16[4,1024,128]{2,1,0:T(8,128)(2,1)}), bf16[4,1024,128]{2,1,0:T(8,128)(2,1)S(1)}, u32[]{:S(2)}, u32[]{:S(2)}) %all-to-all-start.1) | async-done | bytes 1048608 | tf_op jit(solution)/shard_map/all_to_all | solution.py:15
  43.6 1.1 convolution_convert_fusion
  44.7 0.9 broadcast_in_dim.86
  45.6 4.2 %all-to-all-start.2 = ((bf16[32,64,128]{2,1,0:T(8,128)(2,1)}), bf16[32,64,128]{2,1,0:T(8,128)(2,1)S(1)}, u32[]{:S(2)}, u32[]{:S(2)}) async-start(bf16[32,64,128]{2,1,0:T(8,128)(2,1)} %broadcast_in_dim.86), calls=%async_computation.2 | async-start | bytes 1048576 | tf_op jit(solution)/shard_map/all_to_all | solution.py:15
  49.8 0.0 copy-done.2
  49.9 0.1 copy.42
  50.0 0.0 copy-done.3
  50.0 0.1 copy.44
  50.7 6.5 %copy.40 = bf16[1,512,4096]{1,2,0:T(8,128)(2,1)} copy(bf16[1,512,4096]{2,1,0:T(8,128)(2,1)} %param.12) | data formatting | bytes 8388608 | tf_op args[3]
  57.2 6.5 %copy.45 = bf16[1,512,4096]{1,2,0:T(8,128)(2,1)} copy(bf16[1,512,4096]{2,1,0:T(8,128)(2,1)} %param.14) | data formatting | bytes 8388608 | tf_op args[5]
  63.7 0.1 broadcast_in_dim.87
  63.8 0.1 broadcast_in_dim.90
  64.0 0.0 all-to-all-done.2
  64.0 0.3 copy.39
  64.4 0.4 reshape.91
  64.8 4.2 %bitcast_reduce_fusion = (f32[64,64]{0,1:T(8,128)S(1)}, f32[64,64,512]{2,1,0:T(8,128)S(1)}) fusion(f32[64,512]{1,0:T(8,128)S(1)} %get-tuple-element.30, pred[512]{0:T(512)(128)(4,1)S(1)} %add_compare_fusion, bf16[512,64,64]{0,2,1:T(8,128)(2,1)} %bitcast.83, bf16[64,64,64]{2,1,0:T(8,128)(2,1)S(1)} %reshape.91), kind=kOutput, calls=%fused_computation.1 | convolution fusion | flops 274722816 | bytes 13255168 | tf_op jit(solution)/shard_map/while/body/eval_jaxpr/qhd,khd->qhk/dot_general | solution.py:90
  68.9 0.0 copy-start
  69.0 3.2 %copy-done = f32[64,64,512]{2,1,0:T(8,128)} copy-done((f32[64,64,512]{2,1,0:T(8,128)}, f32[64,64,512]{2,1,0:T(8,128)S(1)}, u32[]{:S(2)}) %copy-start) | copy-done | bytes 8388632
  72.2 2.8 %fusion.2 = f32[64,64]{0,1:T(8,128)S(1)} fusion(f32[64,64,512]{2,1,0:T(8,128)S(1)} %get-tuple-element.28, f32[64,64]{0,1:T(8,128)S(1)} %get-tuple-element.27, f32[64,512]{1,0:T(8,128)S(1)} %get-tuple-element.30, pred[512]{0:T(512)(128)(4,1)S(1)} %add_compare_fusion), kind=kLoop, calls=%fused_computation.6 | loop fusion | flops 10481664 | bytes 8552960 | tf_op jit(solution)/shard_map/while/body/eval_jaxpr/reduce_sum | solution.py:100
  75.0 0.7 pad_maximum_fusion
  75.7 8.5 %all-to-all-start.4 = ((f32[1,128,64]{1,0,2:T(1,128)}), f32[1,128,64]{1,0,2:T(1,128)S(1)}, u32[]{:S(2)}, u32[]{:S(2)}) async-start(f32[1,128,64]{1,0,2:T(1,128)} %pad_maximum_fusion), calls=%async_computation.4 | async-start | bytes 65536 | tf_op jit(solution)/shard_map/all_to_all | solution.py:32
  84.2 8.5 %fusion.12 = f32[64,64,64]{2,0,1:T(8,128)} fusion(bf16[512,64,64]{0,2,1:T(8,128)(2,1)} %bitcast.86, f32[64,64,512]{2,1,0:T(8,128)} %copy-done, f32[64,512]{1,0:T(8,128)S(1)} %get-tuple-element.29, f32[64,64]{0,1:T(8,128)S(1)} %get-tuple-element.27, f32[64,512]{1,0:T(8,128)S(1)} %get-tuple-element.30, pred[512]{0:T(512)(128)(4,1)S(1)} %add_compare_fusion), kind=kOutput, calls=%fused_computation.17 | convolution fusion | flops 281018368 | bytes 13910528 | tf_op jit(solution)/shard_map/while/body/eval_jaxpr/qhk,khd->qhd/dot_general | solution.py:102
  92.8 0.0 copy-start.1
  92.8 2.0 %copy.50 = f32[64,64,64]{0,2,1:T(8,128)S(1)} copy(f32[64,64,64]{2,0,1:T(8,128)} %fusion.12) | data formatting | bytes 2097152 | tf_op jit(solution)/shard_map/while/body/jit(dynamic_update_index_in_dim)/broadcast_in_dim | solution.py:108
  94.7 0.5 broadcast.48
  95.2 19.4 %reduce.3 = f32[4096,64]{1,0:T(8,128)} reduce(f32[4096,1,64]{2,1,0:T(1,128)S(1)} %bitcast.84, f32[]{:T(128)} %broadcast.48), dimensions={1}, to_apply=%bitcast.73.reduce_sub_computation | reduce | bytes 2097156
  114.6 3.4 %reshape.98 = f32[32,1,8192]{2,1,0:T(1,128)} reshape(f32[4096,64]{1,0:T(8,128)} %reduce.3) | data formatting | bytes 2097152
  118.1 0.0 all-to-all-done.4
  118.1 8.1 %all-to-all-start.3 = ((f32[32,1,8192]{2,1,0:T(1,128)}), f32[32,1,8192]{2,1,0:T(1,128)S(1)}, u32[]{:S(2)}, u32[]{:S(2)}) async-start(f32[32,1,8192]{2,1,0:T(1,128)} %reshape.98), calls=%async_computation.3 | async-start | bytes 2097152 | tf_op jit(solution)/shard_map/all_to_all | solution.py:118
  126.2 0.0 copy-done.1
  126.2 0.2 copy.49
  126.4 15.4 %all-to-all-done.3 = f32[32,1,8192]{2,1,0:T(1,128)S(1)} async-done(((f32[32,1,8192]{2,1,0:T(1,128)}), f32[32,1,8192]{2,1,0:T(1,128)S(1)}, u32[]{:S(2)}, u32[]{:S(2)}) %all-to-all-start.3) | async-done | bytes 1048608 | tf_op jit(solution)/shard_map/all_to_all | solution.py:118
  141.8 1.2 broadcast_in_dim.94
  142.9 4.5 %all-to-all-start.5 = ((bf16[4,128,1024]{1,2,0:T(8,128)(2,1)}), bf16[4,128,1024]{1,2,0:T(8,128)(2,1)}, u32[]{:S(2)}, u32[]{:S(2)}) async-start(bf16[4,128,1024]{1,2,0:T(8,128)(2,1)} %broadcast_in_dim.94), calls=%async_computation.5 | async-start | bytes 2097152 | tf_op jit(solution)/shard_map/all_to_all | solution.py:15
  147.4 0.1 fusion.21
  147.6 3.2 %reduce.4 = f32[32,8192]{1,0:T(8,128)S(1)} reduce(f32[32,1,8192]{2,1,0:T(1,128)S(1)} %all-to-all-done.3, f32[]{:T(128)} %broadcast.48), dimensions={1}, to_apply=%all_to_all.42.reduce_sub_computation | reduce | bytes 2097156 | tf_op jit(solution)/shard_map/all_to_all | solution.py:118
  150.8 2.6 %reshape.99 = f32[4096,1,64]{2,1,0:T(1,128)S(1)} reshape(f32[32,8192]{1,0:T(8,128)S(1)} %reduce.4) | data formatting | bytes 2097152
  153.4 0.3 fusion.11
  153.7 9.5 %all-to-all-done.5 = bf16[4,128,1024]{1,2,0:T(8,128)(2,1)} async-done(((bf16[4,128,1024]{1,2,0:T(8,128)(2,1)}), bf16[4,128,1024]{1,2,0:T(8,128)(2,1)}, u32[]{:S(2)}, u32[]{:S(2)}) %all-to-all-start.5) | async-done | bytes 1048608 | tf_op jit(solution)/shard_map/all_to_all | solution.py:15
  163.2 1.7 convolution_bitcast_fusion
  164.9 20.9 %all_to_all.59 = f32[32,64,128]{2,1,0:T(8,128)S(1)} all-to-all(f32[32,64,128]{2,1,0:T(8,128)S(1)} %convolution_bitcast_fusion), channel_id=1, replica_groups=mesh['seg'=32,'rep'=4] {'seg'}, dimensions={0} | all-to-all | bytes 2097152 | tf_op jit(solution)/shard_map/all_to_all | solution.py:46
  185.8 0.7 reduce_sum.53
  (5 shorter events, 0.1 us)
Async XLA Ops:
  0.0 49.8 %copy-start.2 = (f32[1,4,64]{2,1,0:T(4,128)S(1)}, f32[1,4,64]{2,1,0:T(4,128)}, u32[]{:S(2)}) copy-start(f32[1,4,64]{2,1,0:T(4,128)} %param.13) | copy-start | bytes 3076
  0.0 50.0 %copy-start.3 = (f32[1,4,64]{2,1,0:T(4,128)S(1)}, f32[1,4,64]{2,1,0:T(4,128)}, u32[]{:S(2)}) copy-start(f32[1,4,64]{2,1,0:T(4,128)} %param.15) | copy-start | bytes 3076
  23.5 20.1 %all-to-all-start.1 = ((bf16[4,1024,128]{2,1,0:T(8,128)(2,1)}), bf16[4,1024,128]{2,1,0:T(8,128)(2,1)S(1)}, u32[]{:S(2)}, u32[]{:S(2)}) async-start(bf16[4,1024,128]{2,1,0:T(8,128)(2,1)} %broadcast_in_dim.85), calls=%async_computation.1 | async-start | bytes 2097152 | tf_op jit(solution)/shard_map/all_to_all | solution.py:15
  45.6 18.4 %all-to-all-start.2 = ((bf16[32,64,128]{2,1,0:T(8,128)(2,1)}), bf16[32,64,128]{2,1,0:T(8,128)(2,1)S(1)}, u32[]{:S(2)}, u32[]{:S(2)}) async-start(bf16[32,64,128]{2,1,0:T(8,128)(2,1)} %broadcast_in_dim.86), calls=%async_computation.2 | async-start | bytes 1048576 | tf_op jit(solution)/shard_map/all_to_all | solution.py:15
  68.9 3.2 %copy-start = (f32[64,64,512]{2,1,0:T(8,128)}, f32[64,64,512]{2,1,0:T(8,128)S(1)}, u32[]{:S(2)}) copy-start(f32[64,64,512]{2,1,0:T(8,128)S(1)} %get-tuple-element.28) | copy-start | bytes 25165828
  75.7 42.3 %all-to-all-start.4 = ((f32[1,128,64]{1,0,2:T(1,128)}), f32[1,128,64]{1,0,2:T(1,128)S(1)}, u32[]{:S(2)}, u32[]{:S(2)}) async-start(f32[1,128,64]{1,0,2:T(1,128)} %pad_maximum_fusion), calls=%async_computation.4 | async-start | bytes 65536 | tf_op jit(solution)/shard_map/all_to_all | solution.py:32
  92.8 33.5 %copy-start.1 = (bf16[128,1024]{1,0:T(8,128)(2,1)S(1)}, bf16[128,1024]{1,0:T(8,128)(2,1)}, u32[]{:S(2)}) copy-start(bf16[128,1024]{1,0:T(8,128)(2,1)} %param.17) | copy-start | bytes 786436
  118.1 23.7 %all-to-all-start.3 = ((f32[32,1,8192]{2,1,0:T(1,128)}), f32[32,1,8192]{2,1,0:T(1,128)S(1)}, u32[]{:S(2)}, u32[]{:S(2)}) async-start(f32[32,1,8192]{2,1,0:T(1,128)} %reshape.98), calls=%async_computation.3 | async-start | bytes 2097152 | tf_op jit(solution)/shard_map/all_to_all | solution.py:118
  142.9 20.2 %all-to-all-start.5 = ((bf16[4,128,1024]{1,2,0:T(8,128)(2,1)}), bf16[4,128,1024]{1,2,0:T(8,128)(2,1)}, u32[]{:S(2)}, u32[]{:S(2)}) async-start(bf16[4,128,1024]{1,2,0:T(8,128)(2,1)} %broadcast_in_dim.94), calls=%async_computation.5 | async-start | bytes 2097152 | tf_op jit(solution)/shard_map/all_to_all | solution.py:15
where the time goes:
time: 188 us; the launch traced here: 186 us
  blocking collectives  41.5 us (22%)
  waiting for transfers between devices  40.6 us (22%)
  local copies, waits for them, and re-layouts  31.1 us (17%)
  starting transfers between devices  29.5 us (16%)
  other arithmetic  27.5 us (15%)
  matrix products  15.5 us (8%)
    all_to_all x3, waiting for transfers between devices, from_everyone(): lax.all_to_all(jnp.broadcast_to(shard[None], (count, *shard.shape)), axis...  25.2 us
    unnamed x14, local copies, waits for them, and re-layouts  23 us
    all_to_all x1, blocking collectives, sent_and_summed(): lax.all_to_all(tiles, axis, split_axis=0, concat_axis=0, tiled=True)  20.9 us
    all_to_all x1, blocking collectives, from_everyone(): lax.all_to_all(jnp.broadcast_to(shard[None], (count, *shard.shape)), axis...  20.6 us
    unnamed x1, other arithmetic  19.4 us
    all_to_all x1, waiting for transfers between devices, per_device(): lax.all_to_all(outputs[None], 'seg', split_axis=2, concat_axis=0, tiled=T...  15.4 us
    all_to_all x3, starting transfers between devices, from_everyone(): lax.all_to_all(jnp.broadcast_to(shard[None], (count, *shard.shape)), axis...  12.8 us
    dot_general x1, matrix products, one_doc(): jnp.einsum('qhk,khd->qhd', scaled, split_values, preferred_element_type=j...  8.53 us
  transfers between devices with their start and end apart: 5, of which 3 were waited for; matrix products, arithmetic and copies ran while one was open for 29% of the time, Pallas kernels for 0%

commit v1 on v0

v1 whole, which is shorter than its diff:
```python
import functools
import math

import jax
import jax.numpy as jnp
from jax import lax
from jax.experimental import pallas as pl
from jax.experimental.pallas import tpu as pltpu
from jax.sharding import PartitionSpec as P

LOG2E = math.log2(math.e)
BF16, F32 = jnp.bfloat16, jnp.float32
LANES = 128
STAT_ROWS = 8
EMPTY = -1e30
VMEM = pl.BlockSpec(memory_space=pltpu.VMEM)
SMEM = pl.BlockSpec(memory_space=pltpu.SMEM)


def params(mib):
    return pltpu.CompilerParams(vmem_limit_bytes=mib << 20)


def cost(flops, moved):
    return pl.CostEstimate(flops=flops, bytes_accessed=moved, transcendentals=0)


def flip_pair(block):
    half = block.shape[0]
    turned = jnp.concatenate([block, block], axis=0).T
    left = lax.broadcasted_iota(jnp.int32, block.shape, 1) < half
    return jnp.where(left, turned[:half], turned[half:])


def query_kernel(rep_ref, x_ref, gain_ref, *refs):
    weights, out_ref = refs[:-1], refs[-1]
    segs, rows, _ = x_ref.shape
    each = segs // len(weights)
    squares = jnp.zeros((rows, LANES), F32)
    for j in range(segs):
        wide = x_ref[j].astype(F32)
        squares += wide * wide
    mean = jnp.sum(squares, axis=1, keepdims=True) * (1.0 / (segs * LANES))
    scale = lax.rsqrt(mean + 1e-06)
    total = jnp.zeros((rows, LANES), F32)
    for i, w_ref in enumerate(weights):
        first = (rep_ref[0] ^ i) * each
        for j in range(0, each, 2):
            pair = [
                (x_ref[first + k].astype(F32) * scale * gain_ref[pl.ds(first + k, 1), :]).astype(BF16)
                for k in (j, j + 1)
            ]
            total += jnp.dot(
                jnp.concatenate(pair, axis=1),
                w_ref[j * LANES : (j + 2) * LANES, :],
                preferred_element_type=F32,
            )
    own = flip_pair(total).astype(BF16)
    for j in range(segs):
        out_ref[j] = own


def turn_kernel(v_ref, out_ref):
    out_ref[...] = v_ref[...].T


def attend_kernel(used_ref, q_ref, k_ref, vt_ref, ks_ref, vs_ref, out_ref):
    segs = q_ref.shape[0]
    half = q_ref.shape[1]
    tokens = k_ref.shape[0]
    blocks = ks_ref.shape[0]
    each = tokens // blocks
    wide = 2 * LANES
    used = used_ref[0]
    sub = lax.broadcasted_iota(jnp.int32, (STAT_ROWS, LANES), 0)
    left = lax.broadcasted_iota(jnp.int32, (half, LANES), 1) < half

    def put(pair, sums, log_sum):
        out_ref[pair, 0:half, :] = sums.astype(BF16)
        high = log_sum.astype(BF16).astype(F32)
        mid = (log_sum - high).astype(BF16).astype(F32)
        low = log_sum - high - mid
        stats = jnp.where(sub == 0, high, jnp.where(sub == 1, mid, jnp.where(sub == 2, low, 0.0)))
        out_ref[pair, half : half + STAT_ROWS, :] = stats.astype(BF16)

    @pl.when(used <= 0)
    def _():
        for pair in range(segs):
            put(pair, jnp.zeros((half, LANES), F32), jnp.full((1, LANES), EMPTY, F32))

    @pl.when(used > 0)
    def _():
        def group(g, carry):
            lanes = pl.ds(pl.multiple_of(g * wide, wide), wide)
            none = jnp.zeros((half, LANES), BF16)
            q0, q1 = q_ref[2 * g], q_ref[2 * g + 1]
            placed = jnp.concatenate(
                [
                    jnp.concatenate([jnp.where(left, q0, none), none], axis=1),
                    jnp.concatenate([jnp.where(left, none, q0), none], axis=1),
                    jnp.concatenate([none, jnp.where(left, q1, none)], axis=1),
                    jnp.concatenate([none, jnp.where(left, none, q1)], axis=1),
                ],
                axis=0,
            )
            scores = []
            for b in range(blocks):
                part = jnp.dot(
                    k_ref[b * each : (b + 1) * each, lanes], placed, preferred_element_type=F32
                )
                part = part * ks_ref[b : b + 1, lanes]
                place = b * each + lax.broadcasted_iota(jnp.int32, part.shape, 0)
                scores.append(jnp.where(place < used, part, EMPTY))
            peak = functools.reduce(jnp.maximum, [jnp.max(p, axis=0, keepdims=True) for p in scores])
            total = jnp.zeros((1, wide), F32)
            scaled = []
            for b in range(blocks):
                weight = jnp.exp2(scores[b] - peak)
                total += jnp.sum(weight, axis=0, keepdims=True)
                scaled.append((weight * vs_ref[b : b + 1, lanes]).astype(BF16))
            sums = jnp.dot(
                vt_ref[pl.ds(pl.multiple_of(g * wide, wide), wide), :],
                jnp.concatenate(scaled, axis=0),
                preferred_element_type=F32,
            )
            inverse = 1.0 / total
            log_sum = peak + jnp.log2(total)
            for i in range(2):
                at = slice(i * LANES, (i + 1) * LANES)
                mine = jnp.where(
                    left,
                    sums[i * LANES : i * LANES + half, at],
                    sums[i * LANES + half : (i + 1) * LANES, at],
                )
                put(2 * g + i, mine * inverse[:, at], log_sum[:, at])
            return carry

        lax.fori_loop(0, segs // 2, group, 0)


def output_kernel(rep_ref, part_ref, *refs):
    weights, out_ref = refs[:-1], refs[-1]
    segs = part_ref.shape[0]
    half = part_ref.shape[1] - STAT_ROWS
    log_sum = jnp.sum(part_ref[:, half : half + STAT_ROWS, :].astype(F32), axis=1)
    share = jnp.exp2(log_sum - jnp.max(log_sum, axis=0, keepdims=True))
    share = share / jnp.sum(share, axis=0, keepdims=True)
    total = jnp.zeros((half, LANES), F32)
    for j in range(segs):
        total += part_ref[j, 0:half, :].astype(F32) * share[j : j + 1, :]
    attended = flip_pair(total).astype(BF16)
    each = segs // len(weights)
    for i, w_ref in enumerate(weights):
        first = (rep_ref[0] ^ i) * each
        update = jnp.dot(attended, w_ref[...], preferred_element_type=F32)
        for j in range(each):
            out_ref[first + j] = update[:, j * LANES : (j + 1) * LANES].astype(BF16)


def sum_kernel(part_ref, out_ref):
    total = part_ref[0].astype(F32)
    for j in range(1, part_ref.shape[0]):
        total += part_ref[j].astype(F32)
    out_ref[...] = total.astype(BF16)


def over_rep(block):
    core = [(0, 1), (1, 0), (2, 3), (3, 2)]
    chip = [(0, 2), (1, 3), (2, 0), (3, 1)]
    far = lax.ppermute(block, "rep", chip)
    near = lax.ppermute(block, "rep", core)
    return block, near, far, lax.ppermute(far, "rep", core)


def swapped(blocks):
    return lax.all_to_all(blocks, "seg", split_axis=0, concat_axis=0, tiled=True)


def per_device(
    decoder_rows,
    norm_gain,
    query_weight,
    key_codes,
    key_scale,
    value_codes,
    value_scale,
    enc_lengths,
    output_weight,
):
    segs = lax.axis_size("seg")
    rows, own = decoder_rows.shape
    _, tokens, inner = key_codes.shape
    blocks, heads = key_scale.shape[1:]
    head_dim = inner // heads
    rep = lax.axis_index("rep").astype(jnp.int32).reshape(1)
    used = jnp.clip(enc_lengths - lax.axis_index("seg") * tokens, 0, tokens).astype(jnp.int32)
    gain = norm_gain.reshape(segs, own)
    key_lanes = jnp.repeat(key_scale[0] * LOG2E, head_dim, axis=1)
    value_lanes = jnp.repeat(value_scale[0], head_dim, axis=1)

    query_blocks = over_rep(query_weight)
    x_all = swapped(jnp.broadcast_to(decoder_rows[None], (segs, rows, own)))
    query_sent = pl.pallas_call(
        query_kernel,
        out_shape=jax.ShapeDtypeStruct((segs, head_dim, LANES), BF16),
        in_specs=[SMEM] + [VMEM] * 6,
        out_specs=VMEM,
        compiler_params=params(16),
        cost_estimate=cost(2 * rows * inner * own, 2 << 20),
        name="query",
    )(rep, x_all, gain, *query_blocks)
    queries = swapped(query_sent)

    turn = 512
    values_t = pl.pallas_call(
        turn_kernel,
        grid=(inner // turn,),
        out_shape=jax.ShapeDtypeStruct((inner, tokens), BF16),
        in_specs=[pl.BlockSpec((tokens, turn), lambda i: (0, i))],
        out_specs=pl.BlockSpec((turn, tokens), lambda i: (i, 0)),
        compiler_params=params(16),
        cost_estimate=cost(2 * inner * tokens * 512, 8 << 20),
        name="turn",
    )(value_codes[0])

    parts = pl.pallas_call(
        attend_kernel,
        out_shape=jax.ShapeDtypeStruct((segs, head_dim + STAT_ROWS, LANES), BF16),
        in_specs=[SMEM] + [VMEM] * 5,
        out_specs=VMEM,
        compiler_params=params(28),
        cost_estimate=cost(16 * rows * inner * tokens, 9 << 20),
        name="attend",
    )(used, queries, key_codes[0], values_t, key_lanes, value_lanes)
    parts = swapped(parts)

    output_blocks = over_rep(output_weight)
    sent = pl.pallas_call(
        output_kernel,
        out_shape=jax.ShapeDtypeStruct((segs, rows, own), BF16),
        in_specs=[SMEM] + [VMEM] * 5,
        out_specs=VMEM,
        compiler_params=params(16),
        cost_estimate=cost(2 * rows * inner * own, 2 << 20),
        name="output",
    )(rep, parts, *output_blocks)
    return pl.pallas_call(
        sum_kernel,
        out_shape=jax.ShapeDtypeStruct((rows, own), BF16),
        in_specs=[VMEM],
        out_specs=VMEM,
        compiler_params=params(8),
        name="gather_sum",
    )(swapped(sent))


def solution(mesh):
    placed = (
        P("rep", "seg"),
        P(),
        P("rep", "seg"),
        P("rep", "seg", None),
        P("rep", "seg", None),
        P("rep", "seg", None),
        P("rep", "seg", None),
        P("rep"),
        P("seg", "rep"),
    )
    return jax.shard_map(
        per_device, mesh=mesh, in_specs=placed, out_specs=P("rep", "seg"), check_vma=False
    )
```

time: 188 us -> 95.5 us (0.51)
  other arithmetic: 27.5 us -> 0.01 us
  blocking collectives: 41.5 us -> 18.4 us
  local copies, waits for them, and re-layouts: 31.1 us -> 12.2 us
  matrix products: 15.5 us -> 0 us
  Pallas kernels: 0 us -> 14.2 us
  waiting for transfers between devices: 40.6 us -> 27.6 us
  starting transfers between devices: 29.5 us -> 22.5 us
    all_to_all x5 -> x3, waiting for transfers between devices: 40.6 us -> 12.6 us  [swapped(): lax.all_to_all(blocks, 'seg', split_axis=0, concat_axis=0, tiled=True)]
    all_to_all x2 -> x1, blocking collectives: 41.5 us -> 18.4 us  [swapped(): lax.all_to_all(blocks, 'seg', split_axis=0, concat_axis=0, tiled=True)]
    unnamed x1 -> x0, other arithmetic: 19.4 us -> none
    dot_general x4 -> x0, matrix products: 15.5 us -> none  [the longest x1 8.53 us: one_doc(): jnp.einsum('qhk,khd->qhd', scaled, split_values, preferred_element_type=j...]
    ppermute x0 -> x6, waiting for transfers between devices: none -> 15 us  [the longest x2 12.2 us: over_rep(): far = lax.ppermute(block, 'rep', chip)]
    pallas_call x0 -> x5, Pallas kernels: none -> 14.2 us  [the longest x1 9.75 us: per_device(): pl.pallas_call(attend_kernel, out_shape=jax.ShapeDtypeStruct((segs, head_...]
    all_to_all x5 -> x3, starting transfers between devices: 29.5 us -> 16.4 us  [swapped(): lax.all_to_all(blocks, 'seg', split_axis=0, concat_axis=0, tiled=True)]
    unnamed x14 -> x18, local copies, waits for them, and re-layouts: 23 us -> 10.2 us
  transfers between devices with their start and end apart: 5 -> 9, of which waited for: 3 -> 5; matrix products, arithmetic and copies ran while one was open for 29% -> 2% of each run, Pallas kernels for 0% -> 2%
where the time goes in v1:
time: 95.5 us; the launch traced here: 95.6 us
  waiting for transfers between devices  27.6 us (29%)
  starting transfers between devices  22.5 us (24%)
  blocking collectives  18.4 us (19%)
  Pallas kernels  14.2 us (15%)
  local copies, waits for them, and re-layouts  12.2 us (13%)
    all_to_all x1, blocking collectives, swapped(): lax.all_to_all(blocks, 'seg', split_axis=0, concat_axis=0, tiled=True)  18.4 us
    all_to_all x3, starting transfers between devices, swapped(): lax.all_to_all(blocks, 'seg', split_axis=0, concat_axis=0, tiled=True)  16.4 us
    all_to_all x3, waiting for transfers between devices, swapped(): lax.all_to_all(blocks, 'seg', split_axis=0, concat_axis=0, tiled=True)  12.6 us
    ppermute x2, waiting for transfers between devices, over_rep(): far = lax.ppermute(block, 'rep', chip)  12.2 us
    unnamed x18, local copies, waits for them, and re-layouts  10.2 us
    pallas_call x1, Pallas kernels, per_device(): pl.pallas_call(attend_kernel, out_shape=jax.ShapeDtypeStruct((segs, head_...  9.75 us
    ppermute x2, starting transfers between devices, over_rep(): far = lax.ppermute(block, 'rep', chip)  5.51 us
  transfers between devices with their start and end apart: 9, of which 5 were waited for; matrix products, arithmetic and copies ran while one was open for 2% of the time, Pallas kernels for 2%

profile of v1, /device:TPU:0, one launch (start us, length us, event | category | flops | bytes accessed | tf_op | source)
XLA Modules:
  0.0 95.6 jit_solution(13952189851148291688)
XLA Ops:
  0.0 0.0 copy-start.8
  0.0 0.0 copy-start.7
  0.0 3.3 %collective-permute-start.1 = (bf16[1024,128]{1,0:T(8,128)(2,1)}, bf16[1024,128]{1,0:T(8,128)(2,1)S(1)}, u32[]{:S(2)}, u32[]{:S(2)}) collective-permute-start(bf16[1024,128]{1,0:T(8,128)(2,1)} %refs_0_.2), channel_id=1, source_target_pairs={{0,2},{1,3},{2,0},{3,1},{4,6},{5,7},{6,4},{7,5},{8,10},{9,11},{10,... | collective-permute-start | bytes 786440 | tf_op jit(solution)/shard_map/ppermute | solution.py:170
  3.3 1.6 %broadcast_in_dim.12 = bf16[32,64,128]{2,1,0:T(8,128)(2,1)} broadcast(bf16[64,128]{1,0:T(8,128)(2,1)} %param.9), dimensions={1,2} | broadcast | bytes 540672 | tf_op jit(solution)/shard_map/broadcast_in_dim | solution.py:202
  4.9 8.3 %all-to-all-start = ((bf16[32,64,128]{2,1,0:T(8,128)(2,1)}), bf16[32,64,128]{2,1,0:T(8,128)(2,1)S(1)}, u32[]{:S(2)}, u32[]{:S(2)}) async-start(bf16[32,64,128]{2,1,0:T(8,128)(2,1)} %broadcast_in_dim.12), calls=%async_computation | async-start | bytes 1048576 | tf_op jit(solution)/shard_map/all_to_all | solution.py:176
  13.2 0.1 collective-permute-start
  13.3 0.0 collective-permute-done.1.refs_2_
  13.3 0.5 collective-permute-start.2
  13.8 1.2 %collective-permute-done.refs_1_ = bf16[1024,128]{1,0:T(8,128)(2,1)S(1)} collective-permute-done((bf16[1024,128]{1,0:T(8,128)(2,1)}, bf16[1024,128]{1,0:T(8,128)(2,1)S(1)}, u32[]{:S(2)}, u32[]{:S(2)}) %collective-permute-start) | collective-permute-done | bytes 262176 | tf_op jit(solution)/shard_map/ppermute | solution.py:171
  15.0 9.4 %all-to-all-done.x_ref = bf16[32,64,128]{2,1,0:T(8,128)(2,1)S(1)} async-done(((bf16[32,64,128]{2,1,0:T(8,128)(2,1)}), bf16[32,64,128]{2,1,0:T(8,128)(2,1)S(1)}, u32[]{:S(2)}, u32[]{:S(2)}) %all-to-all-start) | async-done | bytes 524320 | tf_op jit(solution)/shard_map/all_to_all | solution.py:176
  24.4 0.0 collective-permute-done.2.refs_3_
  24.5 0.0 copy-start.4
  24.5 0.9 copy-done.4
  25.4 0.0 copy-start.6
  25.4 0.7 copy-done.6
  26.1 1.3 %query.1 = bf16[32,64,128]{2,1,0:T(8,128)(2,1)} custom-call(s32[1]{0:T(128)} %bitcast.rep_ref, bf16[32,64,128]{2,1,0:T(8,128)(2,1)S(1)} %all-to-all-done.x_ref, f32[32,128]{1,0:T(8,128)S(1)} %bitcast.10, bf16[1024,128]{1,0:T(8,128)(2,1)S(1)} %copy-done.4, bf16[1024,128]{1,0:T(8,128)(2,1)S(1)} %collective-permute-done.refs_1_, ...), custom_call_target="tpu_custom_call" | custom-call | flops 67108864 | bytes 2097152 | tf_op jit(solution)/shard_map/query/pallas_call | solution.py:203
  27.5 4.2 %all-to-all-start.1 = ((bf16[32,64,128]{2,1,0:T(8,128)(2,1)}), bf16[32,64,128]{2,1,0:T(8,128)(2,1)S(1)}, u32[]{:S(2)}, u32[]{:S(2)}) async-start(bf16[32,64,128]{2,1,0:T(8,128)(2,1)} %query.1), calls=%async_computation.1 | async-start | bytes 1048576 | tf_op jit(solution)/shard_map/all_to_all | solution.py:176
  32.3 0.0 copy-done.8
  32.4 0.1 broadcast_in_dim.13
  32.5 0.1 reshape.17.ks_ref
  32.6 0.0 copy-done.7
  32.6 0.1 broadcast_in_dim.14
  32.7 0.1 reshape.18.vs_ref
  32.8 0.0 copy-start.3
  32.8 2.2 %copy-done.3 = bf16[1,512,4096]{2,1,0:T(8,128)(2,1)S(1)} copy-done((bf16[1,512,4096]{2,1,0:T(8,128)(2,1)S(1)}, bf16[1,512,4096]{2,1,0:T(8,128)(2,1)}, u32[]{:S(2)}) %copy-start.3) | copy-done | bytes 4194328
  35.0 1.9 %turn.1.vt_ref = bf16[4096,512]{1,0:T(8,128)(2,1)S(1)} custom-call(bf16[512,4096]{1,0:T(8,128)(2,1)S(1)} %bitcast.9), custom_call_target="tpu_custom_call" | custom-call | flops 2147483648 | bytes 8388608 | tf_op jit(solution)/shard_map/turn/pallas_call | solution.py:215
  36.9 0.0 copy-start
  36.9 1.9 %copy-done = bf16[4096,512]{1,0:T(8,128)(2,1)} copy-done((bf16[4096,512]{1,0:T(8,128)(2,1)}, bf16[4096,512]{1,0:T(8,128)(2,1)S(1)}, u32[]{:S(2)}) %copy-start) | copy-done | bytes 4194328
  38.8 3.2 %all-to-all-done.1.q_ref = bf16[32,64,128]{2,1,0:T(8,128)(2,1)S(1)} async-done(((bf16[32,64,128]{2,1,0:T(8,128)(2,1)}), bf16[32,64,128]{2,1,0:T(8,128)(2,1)S(1)}, u32[]{:S(2)}, u32[]{:S(2)}) %all-to-all-start.1) | async-done | bytes 524320 | tf_op jit(solution)/shard_map/all_to_all | solution.py:176
  42.0 0.0 copy-start.1
  42.0 2.2 %copy-done.1 = bf16[4096,512]{1,0:T(8,128)(2,1)S(1)} copy-done((bf16[4096,512]{1,0:T(8,128)(2,1)S(1)}, bf16[4096,512]{1,0:T(8,128)(2,1)}, u32[]{:S(2)}) %copy-start.1) | copy-done | bytes 4194328
  44.2 0.0 copy-start.2
  44.2 2.2 %copy-done.2 = bf16[1,512,4096]{2,1,0:T(8,128)(2,1)S(1)} copy-done((bf16[1,512,4096]{2,1,0:T(8,128)(2,1)S(1)}, bf16[1,512,4096]{2,1,0:T(8,128)(2,1)}, u32[]{:S(2)}) %copy-start.2) | copy-done | bytes 4194328
  46.4 0.0 copy-start.5
  46.4 9.7 %attend.1 = bf16[32,72,128]{2,1,0:T(8,128)(2,1)} custom-call(s32[1]{0:T(128)S(6)} %min.6.used_ref, bf16[32,64,128]{2,1,0:T(8,128)(2,1)S(1)} %all-to-all-done.1.q_ref, bf16[512,4096]{1,0:T(8,128)(2,1)S(1)} %bitcast.8, bf16[4096,512]{1,0:T(8,128)(2,1)S(1)} %copy-done.1, f32[4,4096]{1,0:T(4,128)S(1)} %reshape.17.ks_ref, f32[4,4096]{1,0:T(4,128)S(1)} %reshape.18.vs_ref), custom_call_target="tpu_custom_call" | custom-call | flops 2147483648 | bytes 9437184 | tf_op jit(solution)/shard_map/attend/pallas_call | solution.py:226
  56.2 3.9 %all-to-all-start.2 = ((bf16[32,72,128]{2,1,0:T(8,128)(2,1)}), bf16[32,72,128]{2,1,0:T(8,128)(2,1)S(1)}, u32[]{:S(2)}, u32[]{:S(2)}) async-start(bf16[32,72,128]{2,1,0:T(8,128)(2,1)} %attend.1), calls=%async_computation.2 | async-start | bytes 1179648 | tf_op jit(solution)/shard_map/all_to_all | solution.py:176
  60.1 0.0 copy-done.5
  60.1 2.2 %collective-permute-start.4 = (bf16[128,1024]{1,0:T(8,128)(2,1)S(1)}, bf16[128,1024]{1,0:T(8,128)(2,1)S(1)}, u32[]{:S(2)}, u32[]{:S(2)}) collective-permute-start(bf16[128,1024]{1,0:T(8,128)(2,1)S(1)} %copy-done.5), channel_id=1, source_target_pairs={{0,2},{1,3},{2,0},{3,1},{4,6},{5,7},{6,4},{7,5},{8,10},{9,11},{10,... | collective-permute-start | bytes 786440 | tf_op jit(solution)/shard_map/ppermute | solution.py:170
  62.3 0.0 collective-permute-start.3
  62.3 12.2 %collective-permute-done.4.refs_2_ = bf16[128,1024]{1,0:T(8,128)(2,1)S(1)} collective-permute-done((bf16[128,1024]{1,0:T(8,128)(2,1)S(1)}, bf16[128,1024]{1,0:T(8,128)(2,1)S(1)}, u32[]{:S(2)}, u32[]{:S(2)}) %collective-permute-start.4) | collective-permute-done | bytes 262176 | tf_op jit(solution)/shard_map/ppermute | solution.py:170
  74.5 0.0 collective-permute-start.5
  74.5 0.0 collective-permute-done.3.refs_1_
  74.5 1.5 %collective-permute-done.5.refs_3_ = bf16[128,1024]{1,0:T(8,128)(2,1)S(1)} collective-permute-done((bf16[128,1024]{1,0:T(8,128)(2,1)S(1)}, bf16[128,1024]{1,0:T(8,128)(2,1)S(1)}, u32[]{:S(2)}, u32[]{:S(2)}) %collective-permute-start.5) | collective-permute-done | bytes 262176 | tf_op jit(solution)/shard_map/ppermute | solution.py:172
  76.0 0.0 all-to-all-done.2.part_ref
  76.0 0.5 output.1
  76.5 18.4 %all_to_all.20.part_ref = bf16[32,64,128]{2,1,0:T(8,128)(2,1)S(1)} all-to-all(bf16[32,64,128]{2,1,0:T(8,128)(2,1)S(1)} %output.1), channel_id=1, replica_groups=mesh['seg'=32,'rep'=4] {'seg'}, dimensions={0} | all-to-all | bytes 1048576 | tf_op jit(solution)/shard_map/all_to_all | solution.py:176
  94.9 0.7 gather_sum.1
  (1 shorter events, 0.0 us)
Async XLA Ops:
  0.0 32.3 %copy-start.8 = (f32[1,4,64]{2,1,0:T(4,128)S(1)}, f32[1,4,64]{2,1,0:T(4,128)}, u32[]{:S(2)}) copy-start(f32[1,4,64]{2,1,0:T(4,128)} %param.13) | copy-start | bytes 3076
  0.0 32.6 %copy-start.7 = (f32[1,4,64]{2,1,0:T(4,128)S(1)}, f32[1,4,64]{2,1,0:T(4,128)}, u32[]{:S(2)}) copy-start(f32[1,4,64]{2,1,0:T(4,128)} %param.15) | copy-start | bytes 3076
  0.0 13.3 %collective-permute-start.1 = (bf16[1024,128]{1,0:T(8,128)(2,1)}, bf16[1024,128]{1,0:T(8,128)(2,1)S(1)}, u32[]{:S(2)}, u32[]{:S(2)}) collective-permute-start(bf16[1024,128]{1,0:T(8,128)(2,1)} %refs_0_.2), channel_id=1, source_target_pairs={{0,2},{1,3},{2,0},{3,1},{4,6},{5,7},{6,4},{7,5},{8,10},{9,11},{10,... | collective-permute-start | bytes 786440 | tf_op jit(solution)/shard_map/ppermute | solution.py:170
  4.9 19.5 %all-to-all-start = ((bf16[32,64,128]{2,1,0:T(8,128)(2,1)}), bf16[32,64,128]{2,1,0:T(8,128)(2,1)S(1)}, u32[]{:S(2)}, u32[]{:S(2)}) async-start(bf16[32,64,128]{2,1,0:T(8,128)(2,1)} %broadcast_in_dim.12), calls=%async_computation | async-start | bytes 1048576 | tf_op jit(solution)/shard_map/all_to_all | solution.py:176
  13.2 1.8 %collective-permute-start = (bf16[1024,128]{1,0:T(8,128)(2,1)}, bf16[1024,128]{1,0:T(8,128)(2,1)S(1)}, u32[]{:S(2)}, u32[]{:S(2)}) collective-permute-start(bf16[1024,128]{1,0:T(8,128)(2,1)} %refs_0_.2), channel_id=1, source_target_pairs={{0,1},{1,0},{2,3},{3,2},{4,5},{5,4},{6,7},{7,6},{8,9},{9,8},{10,11... | collective-permute-start | bytes 786440 | tf_op jit(solution)/shard_map/ppermute | solution.py:171
  13.3 11.1 %collective-permute-start.2 = (bf16[1024,128]{1,0:T(8,128)(2,1)S(1)}, bf16[1024,128]{1,0:T(8,128)(2,1)S(1)}, u32[]{:S(2)}, u32[]{:S(2)}) collective-permute-start(bf16[1024,128]{1,0:T(8,128)(2,1)S(1)} %collective-permute-done.1.refs_2_), channel_id=1, source_target_pairs={{0,1},{1,0},{2,3},{3,2},{4,5},{5,4},{6,7},{7,6},{8,9},{9,8},{10,11... | collective-permute-start | bytes 786440 | tf_op jit(solution)/shard_map/ppermute | solution.py:172
  24.5 1.0 copy-start.4
  25.4 0.7 copy-start.6
  27.5 14.6 %all-to-all-start.1 = ((bf16[32,64,128]{2,1,0:T(8,128)(2,1)}), bf16[32,64,128]{2,1,0:T(8,128)(2,1)S(1)}, u32[]{:S(2)}, u32[]{:S(2)}) async-start(bf16[32,64,128]{2,1,0:T(8,128)(2,1)} %query.1), calls=%async_computation.1 | async-start | bytes 1048576 | tf_op jit(solution)/shard_map/all_to_all | solution.py:176
  32.8 2.2 %copy-start.3 = (bf16[1,512,4096]{2,1,0:T(8,128)(2,1)S(1)}, bf16[1,512,4096]{2,1,0:T(8,128)(2,1)}, u32[]{:S(2)}) copy-start(bf16[1,512,4096]{2,1,0:T(8,128)(2,1)} %param.14) | copy-start | bytes 12582916
  36.9 1.9 %copy-start = (bf16[4096,512]{1,0:T(8,128)(2,1)}, bf16[4096,512]{1,0:T(8,128)(2,1)S(1)}, u32[]{:S(2)}) copy-start(bf16[4096,512]{1,0:T(8,128)(2,1)S(1)} %turn.1.vt_ref) | copy-start | bytes 12582916
  42.0 2.2 %copy-start.1 = (bf16[4096,512]{1,0:T(8,128)(2,1)S(1)}, bf16[4096,512]{1,0:T(8,128)(2,1)}, u32[]{:S(2)}) copy-start(bf16[4096,512]{1,0:T(8,128)(2,1)} %copy-done) | copy-start | bytes 12582916
  44.2 2.2 %copy-start.2 = (bf16[1,512,4096]{2,1,0:T(8,128)(2,1)S(1)}, bf16[1,512,4096]{2,1,0:T(8,128)(2,1)}, u32[]{:S(2)}) copy-start(bf16[1,512,4096]{2,1,0:T(8,128)(2,1)} %param.12) | copy-start | bytes 12582916
  46.4 13.7 %copy-start.5 = (bf16[128,1024]{1,0:T(8,128)(2,1)S(1)}, bf16[128,1024]{1,0:T(8,128)(2,1)}, u32[]{:S(2)}) copy-start(bf16[128,1024]{1,0:T(8,128)(2,1)} %refs_0_.3) | copy-start | bytes 786436
  56.2 19.8 %all-to-all-start.2 = ((bf16[32,72,128]{2,1,0:T(8,128)(2,1)}), bf16[32,72,128]{2,1,0:T(8,128)(2,1)S(1)}, u32[]{:S(2)}, u32[]{:S(2)}) async-start(bf16[32,72,128]{2,1,0:T(8,128)(2,1)} %attend.1), calls=%async_computation.2 | async-start | bytes 1179648 | tf_op jit(solution)/shard_map/all_to_all | solution.py:176
  60.1 14.4 %collective-permute-start.4 = (bf16[128,1024]{1,0:T(8,128)(2,1)S(1)}, bf16[128,1024]{1,0:T(8,128)(2,1)S(1)}, u32[]{:S(2)}, u32[]{:S(2)}) collective-permute-start(bf16[128,1024]{1,0:T(8,128)(2,1)S(1)} %copy-done.5), channel_id=1, source_target_pairs={{0,2},{1,3},{2,0},{3,1},{4,6},{5,7},{6,4},{7,5},{8,10},{9,11},{10,... | collective-permute-start | bytes 786440 | tf_op jit(solution)/shard_map/ppermute | solution.py:170
  62.3 12.2 %collective-permute-start.3 = (bf16[128,1024]{1,0:T(8,128)(2,1)S(1)}, bf16[128,1024]{1,0:T(8,128)(2,1)S(1)}, u32[]{:S(2)}, u32[]{:S(2)}) collective-permute-start(bf16[128,1024]{1,0:T(8,128)(2,1)S(1)} %copy-done.5), channel_id=1, source_target_pairs={{0,1},{1,0},{2,3},{3,2},{4,5},{5,4},{6,7},{7,6},{8,9},{9,8},{10,11... | collective-permute-start | bytes 786440 | tf_op jit(solution)/shard_map/ppermute | solution.py:171
  74.5 1.5 %collective-permute-start.5 = (bf16[128,1024]{1,0:T(8,128)(2,1)S(1)}, bf16[128,1024]{1,0:T(8,128)(2,1)S(1)}, u32[]{:S(2)}, u32[]{:S(2)}) collective-permute-start(bf16[128,1024]{1,0:T(8,128)(2,1)S(1)} %collective-permute-done.4.refs_2_), channel_id=1, source_target_pairs={{0,1},{1,0},{2,3},{3,2},{4,5},{5,4},{6,7},{7,6},{8,9},{9,8},{10,11... | collective-permute-start | bytes 786440 | tf_op jit(solution)/shard_map/ppermute | solution.py:172

commit v2 on v1

v2 whole, which is shorter than its diff:
```python
import math

import jax
import jax.numpy as jnp
from jax import lax
from jax.experimental import pallas as pl
from jax.experimental.pallas import tpu as pltpu
from jax.sharding import PartitionSpec as P

LOG2E = math.log2(math.e)
BF16, F32 = jnp.bfloat16, jnp.float32
LANES = 128
STAT_ROWS = 8
SUM_ROWS = 16
EMPTY = -1e30
VMEM = pl.BlockSpec(memory_space=pltpu.VMEM)
SMEM = pl.BlockSpec(memory_space=pltpu.SMEM)
HBM = pl.BlockSpec(memory_space=pltpu.HBM)


def params(mib):
    return pltpu.CompilerParams(vmem_limit_bytes=mib << 20)


def cost(flops, moved):
    return pl.CostEstimate(flops=flops, bytes_accessed=moved, transcendentals=0)


def flip_pair(block):
    half = block.shape[0]
    turned = jnp.concatenate([block, block], axis=0).T
    left = lax.broadcasted_iota(jnp.int32, block.shape, 1) < half
    return jnp.where(left, turned[:half], turned[half:])


def stage_kernel(own_ref, gain_ref, own_out, gain_out):
    own_out[...] = own_ref[...]
    gain_out[...] = gain_ref[...]


def query_kernel(rep_ref, x_ref, gain_ref, *refs):
    weights, out_ref = refs[:-1], refs[-1]
    segs, rows, _ = x_ref.shape
    squares = jnp.zeros((rows, LANES), F32)
    for j in range(segs):
        wide = x_ref[j].astype(F32)
        squares += wide * wide
    mean = jnp.sum(squares, axis=1, keepdims=True) * (1.0 / (segs * LANES))
    scale = lax.rsqrt(mean + 1e-06)
    each = segs // len(weights)
    total = jnp.zeros((rows, LANES), F32)
    for i, w_ref in enumerate(weights):
        first = (rep_ref[0] ^ i) * each
        for j in range(0, each, 2):
            pair = [
                (x_ref[first + k].astype(F32) * scale * gain_ref[pl.ds(first + k, 1), :]).astype(BF16)
                for k in (j, j + 1)
            ]
            total += jnp.dot(
                jnp.concatenate(pair, axis=1),
                w_ref[j * LANES : (j + 2) * LANES, :],
                preferred_element_type=F32,
            )
    own = flip_pair(total).astype(BF16)
    for j in range(segs):
        out_ref[j] = own


def turn_kernel(v_ref, out_ref):
    turned = v_ref[...].T
    shape = (SUM_ROWS, turned.shape[1])
    row = lax.broadcasted_iota(jnp.int32, shape, 0)
    block = lax.broadcasted_iota(jnp.int32, shape, 1) // LANES
    picks = jnp.where(row == block, 1.0, 0.0).astype(BF16)
    for i in range(2):
        out_ref[0, i, 0:LANES, :] = turned[i * LANES : (i + 1) * LANES]
        out_ref[0, i, LANES : LANES + SUM_ROWS, :] = picks


def attend_kernel(
    used_ref, q_ref, ks_ref, lvs_ref, ivs_ref, k_hbm, vt_hbm, out_ref,
    k_buf, vt_buf, s0, s1, p0, p1, m0, m1, n0, n1, k_sems, vt_sems,
):
    groups = vt_hbm.shape[0]
    half = q_ref.shape[1]
    blocks = ks_ref.shape[0]
    wide = 2 * LANES
    used = used_ref[0]
    sub = lax.broadcasted_iota(jnp.int32, (STAT_ROWS, LANES), 0)
    left = lax.broadcasted_iota(jnp.int32, (half, LANES), 1) < half

    def lanes_of(g):
        return pl.ds(g * wide if isinstance(g, int) else pl.multiple_of(g * wide, wide), wide)

    def k_copy(g):
        return pltpu.make_async_copy(k_hbm.at[:, lanes_of(g)], k_buf.at[g], k_sems.at[g])

    def vt_copy(g):
        return pltpu.make_async_copy(vt_hbm.at[g], vt_buf.at[g], vt_sems.at[g])

    for g in range(groups):
        k_copy(g).start()
        vt_copy(g).start()

    def put(pair, sums, log_sum):
        out_ref[pair, 0:half, :] = sums.astype(BF16)
        high = log_sum.astype(BF16).astype(F32)
        mid = (log_sum - high).astype(BF16).astype(F32)
        low = log_sum - high - mid
        stats = jnp.where(sub == 0, high, jnp.where(sub == 1, mid, jnp.where(sub == 2, low, 0.0)))
        out_ref[pair, half : half + STAT_ROWS, :] = stats.astype(BF16)

    def rows_of(b):
        return slice(b * LANES, (b + 1) * LANES)

    def score(g, count, clear, s_ref, m_ref):
        none = jnp.zeros((half, LANES), BF16)
        q0, q1 = q_ref[2 * g], q_ref[2 * g + 1]
        placed = jnp.concatenate(
            [
                jnp.concatenate([jnp.where(left, q0, none), none], axis=1),
                jnp.concatenate([jnp.where(left, none, q0), none], axis=1),
                jnp.concatenate([none, jnp.where(left, q1, none)], axis=1),
                jnp.concatenate([none, jnp.where(left, none, q1)], axis=1),
            ],
            axis=0,
        )
        peak = None
        for b in range(count):
            part = jnp.dot(k_buf[g, rows_of(b), :], placed, preferred_element_type=F32)
            part = part * ks_ref[b : b + 1, lanes_of(g)]
            if b >= clear:
                place = b * LANES + lax.broadcasted_iota(jnp.int32, part.shape, 0)
                part = jnp.where(place < used, part, EMPTY)
            s_ref[rows_of(b), :] = part
            top = jnp.max(part, axis=0, keepdims=True)
            peak = top if peak is None else jnp.maximum(peak, top)
            yield
        m_ref[...] = peak

    def weigh(g, count, s_ref, m_ref, p_ref, n_ref):
        peak = m_ref[...]
        n_ref[...] = peak
        for b in range(count):
            shift = peak - lvs_ref[b : b + 1, lanes_of(g)]
            p_ref[rows_of(b), :] = jnp.exp2(s_ref[rows_of(b), :] - shift).astype(BF16)
            yield

    def gather(g, count, p_ref, n_ref):
        inverse_scale = ivs_ref[:, lanes_of(g)]
        for i in range(2):
            at = rows_of(i)
            sums = jnp.dot(
                vt_buf[g, i, :, 0 : count * LANES],
                p_ref[0 : count * LANES, at],
                preferred_element_type=F32,
            )
            yield
            total = jnp.sum(
                sums[LANES : LANES + count] * inverse_scale[0:count, at], axis=0, keepdims=True
            )
            mine = jnp.where(left, sums[0:half], sums[half:LANES])
            put(2 * g + i, mine * (1.0 / total), n_ref[:, at] + jnp.log2(total))
            yield

    def together(*stages):
        stages = list(stages)
        while stages:
            for stage in list(stages):
                if next(stage, stage) is stage:
                    stages.remove(stage)

    def run(count, clear):
        k_copy(0).wait()
        k_copy(1).wait()
        together(score(0, count, clear, s0, m0))
        together(score(1, count, clear, s1, m1), weigh(0, count, s0, m0, p0, n0))

        def two(i, carry):
            for g in (0, 1):
                k_copy(2 * i + g).wait()
                vt_copy(2 * i - 2 + g).wait()
            together(
                score(2 * i, count, clear, s0, m0),
                gather(2 * i - 2, count, p0, n0),
                weigh(2 * i - 1, count, s1, m1, p1, n1),
            )
            together(
                score(2 * i + 1, count, clear, s1, m1),
                gather(2 * i - 1, count, p1, n1),
                weigh(2 * i, count, s0, m0, p0, n0),
            )
            return carry

        lax.fori_loop(1, groups // 2, two, 0)
        vt_copy(groups - 2).wait()
        vt_copy(groups - 1).wait()
        together(gather(groups - 2, count, p0, n0), weigh(groups - 1, count, s1, m1, p1, n1))
        together(gather(groups - 1, count, p1, n1))

    most = (blocks - 1) * LANES

    @pl.when(used <= 0)
    def _():
        for g in range(groups):
            k_copy(g).wait()
            vt_copy(g).wait()
        for pair in range(2 * groups):
            put(pair, jnp.zeros((half, LANES), F32), jnp.full((1, LANES), EMPTY, F32))

    @pl.when((used > 0) & (used <= most))
    def _():
        run(blocks - 1, 0)

    @pl.when(used > most)
    def _():
        run(blocks, blocks - 1)


def output_kernel(rep_ref, part_ref, *refs):
    weights, out_ref = refs[:-1], refs[-1]
    segs = part_ref.shape[0]
    half = part_ref.shape[1] - STAT_ROWS
    log_sum = jnp.sum(part_ref[:, half : half + STAT_ROWS, :].astype(F32), axis=1)
    share = jnp.exp2(log_sum - jnp.max(log_sum, axis=0, keepdims=True))
    share = share / jnp.sum(share, axis=0, keepdims=True)
    total = jnp.zeros((half, LANES), F32)
    for j in range(segs):
        total += part_ref[j, 0:half, :].astype(F32) * share[j : j + 1, :]
    attended = flip_pair(total).astype(BF16)
    each = segs // len(weights)
    for i, w_ref in enumerate(weights):
        first = (rep_ref[0] ^ i) * each
        update = jnp.dot(attended, w_ref[...], preferred_element_type=F32)
        for j in range(each):
            out_ref[first + j] = update[:, j * LANES : (j + 1) * LANES].astype(BF16)


def sum_kernel(part_ref, out_ref):
    total = part_ref[0].astype(F32)
    for j in range(1, part_ref.shape[0]):
        total += part_ref[j].astype(F32)
    out_ref[...] = total.astype(BF16)


CORE = [(0, 1), (1, 0), (2, 3), (3, 2)]
CHIP = [(0, 2), (1, 3), (2, 0), (3, 1)]


def over_rep(block):
    far = lax.ppermute(block, "rep", CHIP)
    near = lax.ppermute(block, "rep", CORE)
    both = lax.ppermute(far, "rep", CORE)
    return block, near, far, both


def swapped(blocks):
    return lax.all_to_all(blocks, "seg", split_axis=0, concat_axis=0, tiled=True)


def sublayer(
    decoder_rows,
    norm_gain,
    query_weight,
    key_codes,
    key_scale,
    value_codes,
    value_scale,
    enc_lengths,
    output_weight,
):
    segs = lax.axis_size("seg")
    rows, own = decoder_rows.shape
    _, tokens, inner = key_codes.shape
    _, heads = key_scale.shape[1:]
    head_dim = inner // heads
    rep = lax.axis_index("rep").astype(jnp.int32).reshape(1)
    used = jnp.clip(enc_lengths - lax.axis_index("seg") * tokens, 0, tokens).astype(jnp.int32)
    gain = norm_gain.reshape(segs, own)
    key_lanes = jnp.repeat(key_scale[0] * LOG2E, head_dim, axis=1)
    value_logs = jnp.repeat(jnp.log2(value_scale[0]), head_dim, axis=1)
    value_inverse = jnp.repeat(1.0 / value_scale[0], head_dim, axis=1)

    wq, wq_near, wq_far, wq_both = over_rep(query_weight)
    x_all = swapped(jnp.broadcast_to(decoder_rows[None], (segs, rows, own)))
    wq, gain = pl.pallas_call(
        stage_kernel,
        out_shape=(
            jax.ShapeDtypeStruct(wq.shape, BF16),
            jax.ShapeDtypeStruct(gain.shape, F32),
        ),
        in_specs=[VMEM] * 2,
        out_specs=(VMEM, VMEM),
        compiler_params=params(8),
        cost_estimate=cost(1 << 24, 1 << 20),
        name="stage",
    )(wq, gain)
    query_call = pl.pallas_call(
        query_kernel,
        out_shape=jax.ShapeDtypeStruct((segs, head_dim, LANES), BF16),
        in_specs=[SMEM] + [VMEM] * 6,
        out_specs=VMEM,
        compiler_params=params(16),
        cost_estimate=cost(2 * rows * inner * own, 2 << 20),
        name="query",
    )
    query_sent = query_call(rep, x_all, gain, wq, wq_near, wq_far, wq_both)
    queries = swapped(query_sent)

    groups, wide = inner // (2 * LANES), 2 * LANES
    height = LANES + SUM_ROWS
    values_t = pl.pallas_call(
        turn_kernel,
        grid=(groups,),
        out_shape=jax.ShapeDtypeStruct((groups, 2, height, tokens), BF16),
        in_specs=[pl.BlockSpec((tokens, wide), lambda i: (0, i))],
        out_specs=pl.BlockSpec((1, 2, height, tokens), lambda i: (i, 0, 0, 0)),
        compiler_params=params(16),
        cost_estimate=cost(2 * inner * tokens * 512, 8 << 20),
        name="turn",
    )(value_codes[0])

    parts = pl.pallas_call(
        attend_kernel,
        out_shape=jax.ShapeDtypeStruct((segs, head_dim + STAT_ROWS, LANES), BF16),
        in_specs=[SMEM] + [VMEM] * 4 + [HBM] * 2,
        out_specs=VMEM,
        scratch_shapes=[
            pltpu.VMEM((groups, tokens, wide), BF16),
            pltpu.VMEM((groups, 2, height, tokens), BF16),
        ]
        + [pltpu.VMEM((tokens, wide), F32)] * 2
        + [pltpu.VMEM((tokens, wide), BF16)] * 2
        + [pltpu.VMEM((1, wide), F32)] * 4
        + [pltpu.SemaphoreType.DMA((groups,))] * 2,
        compiler_params=params(51),
        cost_estimate=cost(16 * rows * inner * tokens, 9 << 20),
        name="attend",
    )(used, queries, key_lanes, value_logs, value_inverse, key_codes[0], values_t)
    parts = swapped(parts)

    output_blocks = over_rep(output_weight)
    sent = pl.pallas_call(
        output_kernel,
        out_shape=jax.ShapeDtypeStruct((segs, rows, own), BF16),
        in_specs=[SMEM] + [VMEM] * 5,
        out_specs=VMEM,
        compiler_params=params(16),
        cost_estimate=cost(2 * rows * inner * own, 2 << 20),
        name="output",
    )(rep, parts, *output_blocks)
    return pl.pallas_call(
        sum_kernel,
        out_shape=jax.ShapeDtypeStruct((rows, own), BF16),
        in_specs=[VMEM],
        out_specs=VMEM,
        compiler_params=params(8),
        name="gather_sum",
    )(swapped(sent))


def solution(mesh):
    placed = (
        P("rep", "seg"),
        P(),
        P("rep", "seg"),
        P("rep", "seg", None),
        P("rep", "seg", None),
        P("rep", "seg", None),
        P("rep", "seg", None),
        P("rep"),
        P("seg", "rep"),
    )
    return jax.shard_map(
        sublayer, mesh=mesh, in_specs=placed, out_specs=P("rep", "seg"), check_vma=False
    )
```

time: 95.5 us -> 88 us (0.921)
  local copies, waits for them, and re-layouts: 12.2 us -> 8.19 us
  waiting for transfers between devices: 27.6 us -> 23.8 us
  Pallas kernels: 14.2 us -> 11.6 us
  starting transfers between devices: 22.5 us -> 24.6 us
    unnamed x18 -> x14, local copies, waits for them, and re-layouts: 10.2 us -> 5.97 us
    pallas_call x5 -> x6, Pallas kernels: 14.2 us -> 11.6 us  [the longest x1 6.37 us: sublayer(): pl.pallas_call(attend_kernel, out_shape=jax.ShapeDtypeStruct((segs, head_...]
    ppermute x6, waiting for transfers between devices: 15 us -> 12.8 us  [the longest x2 11.2 us: over_rep(): far = lax.ppermute(block, 'rep', CHIP)]
    all_to_all x3, waiting for transfers between devices: 12.6 us -> 11 us  [swapped(): lax.all_to_all(blocks, 'seg', split_axis=0, concat_axis=0, tiled=True)]
    ppermute x6, starting transfers between devices: 6.09 us -> 7.34 us  [the longest x2 6.76 us: over_rep(): far = lax.ppermute(block, 'rep', CHIP)]
  transfers between devices with their start and end apart: 9 -> 9, of which waited for: 5 -> 4; matrix products, arithmetic and copies ran while one was open for 2% -> 3% of each run, Pallas kernels for 2% -> 3%
where the time goes in v2:
time: 88 us; the launch traced here: 87.3 us
  starting transfers between devices  24.6 us (28%)
  waiting for transfers between devices  23.8 us (27%)
  blocking collectives  18.4 us (21%)
  Pallas kernels  11.6 us (13%)
  local copies, waits for them, and re-layouts  8.19 us (9%)
    all_to_all x1, blocking collectives, swapped(): lax.all_to_all(blocks, 'seg', split_axis=0, concat_axis=0, tiled=True)  18.4 us
    all_to_all x3, starting transfers between devices, swapped(): lax.all_to_all(blocks, 'seg', split_axis=0, concat_axis=0, tiled=True)  17.2 us
    ppermute x2, waiting for transfers between devices, over_rep(): far = lax.ppermute(block, 'rep', CHIP)  11.2 us
    all_to_all x3, waiting for transfers between devices, swapped(): lax.all_to_all(blocks, 'seg', split_axis=0, concat_axis=0, tiled=True)  11 us
    ppermute x2, starting transfers between devices, over_rep(): far = lax.ppermute(block, 'rep', CHIP)  6.76 us
    pallas_call x1, Pallas kernels, sublayer(): pl.pallas_call(attend_kernel, out_shape=jax.ShapeDtypeStruct((segs, head_...  6.37 us
    unnamed x14, local copies, waits for them, and re-layouts  5.97 us
    pallas_call x1, Pallas kernels, sublayer(): pl.pallas_call(turn_kernel, grid=(groups,), out_shape=jax.ShapeDtypeStruc...  2.63 us
  transfers between devices with their start and end apart: 9, of which 4 were waited for; matrix products, arithmetic and copies ran while one was open for 3% of the time, Pallas kernels for 3%

profile of v2, /device:TPU:0, one launch (start us, length us, event | category | flops | bytes accessed | tf_op | source)
XLA Modules:
  0.0 87.3 jit_solution(978355099850709207)
XLA Ops:
  0.0 0.0 copy-start.5
  0.0 0.0 copy-start.6
  0.0 3.3 %collective-permute-start.1 = (bf16[1024,128]{1,0:T(8,128)(2,1)}, bf16[1024,128]{1,0:T(8,128)(2,1)S(1)}, u32[]{:S(2)}, u32[]{:S(2)}) collective-permute-start(bf16[1024,128]{1,0:T(8,128)(2,1)} %own_ref.1), channel_id=1, source_target_pairs={{0,2},{1,3},{2,0},{3,1},{4,6},{5,7},{6,4},{7,5},{8,10},{9,11},{10,... | collective-permute-start | bytes 786440 | tf_op jit(solution)/shard_map/ppermute | solution.py:251
  3.3 1.6 %broadcast_in_dim.15 = bf16[32,64,128]{2,1,0:T(8,128)(2,1)} broadcast(bf16[64,128]{1,0:T(8,128)(2,1)} %param.9), dimensions={1,2} | broadcast | bytes 540672 | tf_op jit(solution)/shard_map/broadcast_in_dim | solution.py:285
  4.9 8.3 %all-to-all-start = ((bf16[32,64,128]{2,1,0:T(8,128)(2,1)}), bf16[32,64,128]{2,1,0:T(8,128)(2,1)S(1)}, u32[]{:S(2)}, u32[]{:S(2)}) async-start(bf16[32,64,128]{2,1,0:T(8,128)(2,1)} %broadcast_in_dim.15), calls=%async_computation | async-start | bytes 1048576 | tf_op jit(solution)/shard_map/all_to_all | solution.py:258
  13.2 0.1 collective-permute-start
  13.3 0.0 collective-permute-done.1.refs_2_
  13.3 0.5 collective-permute-start.2
  13.8 0.0 copy-start.3
  13.8 0.9 %copy-done.3 = bf16[1024,128]{1,0:T(8,128)(2,1)S(1)} copy-done((bf16[1024,128]{1,0:T(8,128)(2,1)S(1)}, bf16[1024,128]{1,0:T(8,128)(2,1)}, u32[]{:S(2)}) %copy-start.3) | copy-done | bytes 262168
  14.8 0.0 copy-start.4
  14.8 0.7 copy-done.4
  15.5 0.0 collective-permute-done.refs_1_
  15.5 8.9 %all-to-all-done.x_ref = bf16[32,64,128]{2,1,0:T(8,128)(2,1)S(1)} async-done(((bf16[32,64,128]{2,1,0:T(8,128)(2,1)}), bf16[32,64,128]{2,1,0:T(8,128)(2,1)S(1)}, u32[]{:S(2)}, u32[]{:S(2)}) %all-to-all-start) | async-done | bytes 524320 | tf_op jit(solution)/shard_map/all_to_all | solution.py:258
  24.4 0.0 collective-permute-done.2.refs_3_
  24.5 1.3 %query.1 = bf16[32,64,128]{2,1,0:T(8,128)(2,1)} custom-call(s32[1]{0:T(128)} %bitcast.rep_ref, bf16[32,64,128]{2,1,0:T(8,128)(2,1)S(1)} %all-to-all-done.x_ref, f32[32,128]{1,0:T(8,128)S(1)} %get-tuple-element.7.gain_ref, bf16[1024,128]{1,0:T(8,128)(2,1)S(1)} %get-tuple-element.8.refs_0_, bf16[1024,128]{1,0:T(8,128)(2,1)S(1)} %collective-permute-done.refs_1_, ...), custom_call_target="tpu_custom_call" | custom-call | flops 67108864 | bytes 2097152 | tf_op jit(solution)/shard_map/query/pallas_call | solution.py:307
  25.8 4.2 %all-to-all-start.1 = ((bf16[32,64,128]{2,1,0:T(8,128)(2,1)}), bf16[32,64,128]{2,1,0:T(8,128)(2,1)S(1)}, u32[]{:S(2)}, u32[]{:S(2)}) async-start(bf16[32,64,128]{2,1,0:T(8,128)(2,1)} %query.1), calls=%async_computation.1 | async-start | bytes 1048576 | tf_op jit(solution)/shard_map/all_to_all | solution.py:258
  30.0 0.0 copy-done.5
  30.0 0.1 broadcast_in_dim.17
  30.1 0.1 reshape.26.lvs_ref
  30.2 0.1 broadcast_in_dim.18
  30.3 0.1 reshape.27.ivs_ref
  31.1 0.0 copy-done.6
  31.1 0.1 broadcast_in_dim.16
  31.2 0.1 reshape.25.ks_ref
  31.3 0.0 copy-start.1
  31.4 2.2 %copy-done.1 = bf16[1,512,4096]{2,1,0:T(8,128)(2,1)S(1)} copy-done((bf16[1,512,4096]{2,1,0:T(8,128)(2,1)S(1)}, bf16[1,512,4096]{2,1,0:T(8,128)(2,1)}, u32[]{:S(2)}) %copy-start.1) | copy-done | bytes 4194328
  33.5 2.6 %turn.1.vt_hbm = bf16[16,2,144,512]{3,2,1,0:T(8,128)(2,1)S(1)} custom-call(bf16[512,4096]{1,0:T(8,128)(2,1)S(1)} %bitcast.11), custom_call_target="tpu_custom_call" | custom-call | flops 2147483648 | bytes 8388608 | tf_op jit(solution)/shard_map/turn/pallas_call | solution.py:312
  36.2 0.0 copy-start
  36.2 2.1 %copy-done = bf16[16,2,144,512]{3,2,1,0:T(8,128)(2,1)} copy-done((bf16[16,2,144,512]{3,2,1,0:T(8,128)(2,1)}, bf16[16,2,144,512]{3,2,1,0:T(8,128)(2,1)S(1)}, u32[]{:S(2)}) %copy-start) | copy-done | bytes 4718616
  38.3 2.1 %all-to-all-done.1.q_ref = bf16[32,64,128]{2,1,0:T(8,128)(2,1)S(1)} async-done(((bf16[32,64,128]{2,1,0:T(8,128)(2,1)}), bf16[32,64,128]{2,1,0:T(8,128)(2,1)S(1)}, u32[]{:S(2)}, u32[]{:S(2)}) %all-to-all-start.1) | async-done | bytes 524320 | tf_op jit(solution)/shard_map/all_to_all | solution.py:258
  40.4 0.0 copy-start.2
  40.4 6.4 %attend.1 = bf16[32,72,128]{2,1,0:T(8,128)(2,1)} custom-call(s32[1]{0:T(128)S(6)} %min.6.used_ref, bf16[32,64,128]{2,1,0:T(8,128)(2,1)S(1)} %all-to-all-done.1.q_ref, f32[4,4096]{1,0:T(4,128)S(1)} %reshape.25.ks_ref, f32[4,4096]{1,0:T(4,128)S(1)} %reshape.26.lvs_ref, f32[4,4096]{1,0:T(4,128)S(1)} %reshape.27.ivs_ref, bf16[512,4096]{1,0:T(8,128)(2,1)} %bitcast.13, ...), custom_call_target="tpu_custom_call" | custom-call | flops 2147483648 | bytes 9437184 | tf_op jit(solution)/shard_map/attend/pallas_call | solution.py:323
  46.7 4.7 %all-to-all-start.2 = ((bf16[32,72,128]{2,1,0:T(8,128)(2,1)}), bf16[32,72,128]{2,1,0:T(8,128)(2,1)S(1)}, u32[]{:S(2)}, u32[]{:S(2)}) async-start(bf16[32,72,128]{2,1,0:T(8,128)(2,1)} %attend.1), calls=%async_computation.2 | async-start | bytes 1179648 | tf_op jit(solution)/shard_map/all_to_all | solution.py:258
  51.5 0.0 copy-done.2
  51.5 3.5 %collective-permute-start.4 = (bf16[128,1024]{1,0:T(8,128)(2,1)S(1)}, bf16[128,1024]{1,0:T(8,128)(2,1)S(1)}, u32[]{:S(2)}, u32[]{:S(2)}) collective-permute-start(bf16[128,1024]{1,0:T(8,128)(2,1)S(1)} %copy-done.2), channel_id=1, source_target_pairs={{0,2},{1,3},{2,0},{3,1},{4,6},{5,7},{6,4},{7,5},{8,10},{9,11},{10,... | collective-permute-start | bytes 786440 | tf_op jit(solution)/shard_map/ppermute | solution.py:251
  54.9 0.0 collective-permute-start.3
  54.9 11.2 %collective-permute-done.4.refs_2_ = bf16[128,1024]{1,0:T(8,128)(2,1)S(1)} collective-permute-done((bf16[128,1024]{1,0:T(8,128)(2,1)S(1)}, bf16[128,1024]{1,0:T(8,128)(2,1)S(1)}, u32[]{:S(2)}, u32[]{:S(2)}) %collective-permute-start.4) | collective-permute-done | bytes 262176 | tf_op jit(solution)/shard_map/ppermute | solution.py:251
  66.2 0.0 collective-permute-start.5
  66.2 0.0 collective-permute-done.3.refs_1_
  66.2 1.5 %collective-permute-done.5.refs_3_ = bf16[128,1024]{1,0:T(8,128)(2,1)S(1)} collective-permute-done((bf16[128,1024]{1,0:T(8,128)(2,1)S(1)}, bf16[128,1024]{1,0:T(8,128)(2,1)S(1)}, u32[]{:S(2)}, u32[]{:S(2)}) %collective-permute-start.5) | collective-permute-done | bytes 262176 | tf_op jit(solution)/shard_map/ppermute | solution.py:253
  67.7 0.0 all-to-all-done.2.part_ref
  67.7 0.5 output.1
  68.3 18.4 %all_to_all.20.part_ref = bf16[32,64,128]{2,1,0:T(8,128)(2,1)S(1)} all-to-all(bf16[32,64,128]{2,1,0:T(8,128)(2,1)S(1)} %output.1), channel_id=1, replica_groups=mesh['seg'=32,'rep'=4] {'seg'}, dimensions={0} | all-to-all | bytes 1048576 | tf_op jit(solution)/shard_map/all_to_all | solution.py:258
  86.6 0.7 gather_sum.1
  (3 shorter events, 0.0 us)
Async XLA Ops:
  0.0 30.0 %copy-start.5 = (f32[1,4,64]{2,1,0:T(4,128)S(1)}, f32[1,4,64]{2,1,0:T(4,128)}, u32[]{:S(2)}) copy-start(f32[1,4,64]{2,1,0:T(4,128)} %param.15) | copy-start | bytes 3076
  0.0 31.1 %copy-start.6 = (f32[1,4,64]{2,1,0:T(4,128)S(1)}, f32[1,4,64]{2,1,0:T(4,128)}, u32[]{:S(2)}) copy-start(f32[1,4,64]{2,1,0:T(4,128)} %param.13) | copy-start | bytes 3076
  0.0 13.3 %collective-permute-start.1 = (bf16[1024,128]{1,0:T(8,128)(2,1)}, bf16[1024,128]{1,0:T(8,128)(2,1)S(1)}, u32[]{:S(2)}, u32[]{:S(2)}) collective-permute-start(bf16[1024,128]{1,0:T(8,128)(2,1)} %own_ref.1), channel_id=1, source_target_pairs={{0,2},{1,3},{2,0},{3,1},{4,6},{5,7},{6,4},{7,5},{8,10},{9,11},{10,... | collective-permute-start | bytes 786440 | tf_op jit(solution)/shard_map/ppermute | solution.py:251
  4.9 19.5 %all-to-all-start = ((bf16[32,64,128]{2,1,0:T(8,128)(2,1)}), bf16[32,64,128]{2,1,0:T(8,128)(2,1)S(1)}, u32[]{:S(2)}, u32[]{:S(2)}) async-start(bf16[32,64,128]{2,1,0:T(8,128)(2,1)} %broadcast_in_dim.15), calls=%async_computation | async-start | bytes 1048576 | tf_op jit(solution)/shard_map/all_to_all | solution.py:258
  13.2 2.3 %collective-permute-start = (bf16[1024,128]{1,0:T(8,128)(2,1)}, bf16[1024,128]{1,0:T(8,128)(2,1)S(1)}, u32[]{:S(2)}, u32[]{:S(2)}) collective-permute-start(bf16[1024,128]{1,0:T(8,128)(2,1)} %own_ref.1), channel_id=1, source_target_pairs={{0,1},{1,0},{2,3},{3,2},{4,5},{5,4},{6,7},{7,6},{8,9},{9,8},{10,11... | collective-permute-start | bytes 786440 | tf_op jit(solution)/shard_map/ppermute | solution.py:252
  13.3 11.1 %collective-permute-start.2 = (bf16[1024,128]{1,0:T(8,128)(2,1)S(1)}, bf16[1024,128]{1,0:T(8,128)(2,1)S(1)}, u32[]{:S(2)}, u32[]{:S(2)}) collective-permute-start(bf16[1024,128]{1,0:T(8,128)(2,1)S(1)} %collective-permute-done.1.refs_2_), channel_id=1, source_target_pairs={{0,1},{1,0},{2,3},{3,2},{4,5},{5,4},{6,7},{7,6},{8,9},{9,8},{10,11... | collective-permute-start | bytes 786440 | tf_op jit(solution)/shard_map/ppermute | solution.py:253
  13.8 0.9 %copy-start.3 = (bf16[1024,128]{1,0:T(8,128)(2,1)S(1)}, bf16[1024,128]{1,0:T(8,128)(2,1)}, u32[]{:S(2)}) copy-start(bf16[1024,128]{1,0:T(8,128)(2,1)} %own_ref.1) | copy-start | bytes 786436
  14.8 0.7 copy-start.4
  25.8 14.6 %all-to-all-start.1 = ((bf16[32,64,128]{2,1,0:T(8,128)(2,1)}), bf16[32,64,128]{2,1,0:T(8,128)(2,1)S(1)}, u32[]{:S(2)}, u32[]{:S(2)}) async-start(bf16[32,64,128]{2,1,0:T(8,128)(2,1)} %query.1), calls=%async_computation.1 | async-start | bytes 1048576 | tf_op jit(solution)/shard_map/all_to_all | solution.py:258
  31.3 2.2 %copy-start.1 = (bf16[1,512,4096]{2,1,0:T(8,128)(2,1)S(1)}, bf16[1,512,4096]{2,1,0:T(8,128)(2,1)}, u32[]{:S(2)}) copy-start(bf16[1,512,4096]{2,1,0:T(8,128)(2,1)} %param.14) | copy-start | bytes 12582916
  36.2 2.1 %copy-start = (bf16[16,2,144,512]{3,2,1,0:T(8,128)(2,1)}, bf16[16,2,144,512]{3,2,1,0:T(8,128)(2,1)S(1)}, u32[]{:S(2)}) copy-start(bf16[16,2,144,512]{3,2,1,0:T(8,128)(2,1)S(1)} %turn.1.vt_hbm) | copy-start | bytes 14155780
  40.4 11.1 %copy-start.2 = (bf16[128,1024]{1,0:T(8,128)(2,1)S(1)}, bf16[128,1024]{1,0:T(8,128)(2,1)}, u32[]{:S(2)}) copy-start(bf16[128,1024]{1,0:T(8,128)(2,1)} %refs_0_.1) | copy-start | bytes 786436
  46.7 21.0 %all-to-all-start.2 = ((bf16[32,72,128]{2,1,0:T(8,128)(2,1)}), bf16[32,72,128]{2,1,0:T(8,128)(2,1)S(1)}, u32[]{:S(2)}, u32[]{:S(2)}) async-start(bf16[32,72,128]{2,1,0:T(8,128)(2,1)} %attend.1), calls=%async_computation.2 | async-start | bytes 1179648 | tf_op jit(solution)/shard_map/all_to_all | solution.py:258
  51.5 14.7 %collective-permute-start.4 = (bf16[128,1024]{1,0:T(8,128)(2,1)S(1)}, bf16[128,1024]{1,0:T(8,128)(2,1)S(1)}, u32[]{:S(2)}, u32[]{:S(2)}) collective-permute-start(bf16[128,1024]{1,0:T(8,128)(2,1)S(1)} %copy-done.2), channel_id=1, source_target_pairs={{0,2},{1,3},{2,0},{3,1},{4,6},{5,7},{6,4},{7,5},{8,10},{9,11},{10,... | collective-permute-start | bytes 786440 | tf_op jit(solution)/shard_map/ppermute | solution.py:251
  54.9 11.2 %collective-permute-start.3 = (bf16[128,1024]{1,0:T(8,128)(2,1)S(1)}, bf16[128,1024]{1,0:T(8,128)(2,1)S(1)}, u32[]{:S(2)}, u32[]{:S(2)}) collective-permute-start(bf16[128,1024]{1,0:T(8,128)(2,1)S(1)} %copy-done.2), channel_id=1, source_target_pairs={{0,1},{1,0},{2,3},{3,2},{4,5},{5,4},{6,7},{7,6},{8,9},{9,8},{10,11... | collective-permute-start | bytes 786440 | tf_op jit(solution)/shard_map/ppermute | solution.py:252
  66.2 1.5 %collective-permute-start.5 = (bf16[128,1024]{1,0:T(8,128)(2,1)S(1)}, bf16[128,1024]{1,0:T(8,128)(2,1)S(1)}, u32[]{:S(2)}, u32[]{:S(2)}) collective-permute-start(bf16[128,1024]{1,0:T(8,128)(2,1)S(1)} %collective-permute-done.4.refs_2_), channel_id=1, source_target_pairs={{0,1},{1,0},{2,3},{3,2},{4,5},{5,4},{6,7},{7,6},{8,9},{9,8},{10,11... | collective-permute-start | bytes 786440 | tf_op jit(solution)/shard_map/ppermute | solution.py:253

commit v3 on v2

--- a/solution.py
+++ b/solution.py
@@ -13,6 +13,7 @@
 STAT_ROWS = 8
 SUM_ROWS = 16
 EMPTY = -1e30
+FIRST = 10
 VMEM = pl.BlockSpec(memory_space=pltpu.VMEM)
 SMEM = pl.BlockSpec(memory_space=pltpu.SMEM)
 HBM = pl.BlockSpec(memory_space=pltpu.HBM)
@@ -31,11 +32,6 @@
     turned = jnp.concatenate([block, block], axis=0).T
     left = lax.broadcasted_iota(jnp.int32, block.shape, 1) < half
     return jnp.where(left, turned[:half], turned[half:])
-
-
-def stage_kernel(own_ref, gain_ref, own_out, gain_out):
-    own_out[...] = own_ref[...]
-    gain_out[...] = gain_ref[...]
 
 
 def query_kernel(rep_ref, x_ref, gain_ref, *refs):
@@ -53,7 +49,7 @@
         first = (rep_ref[0] ^ i) * each
         for j in range(0, each, 2):
             pair = [
-                (x_ref[first + k].astype(F32) * scale * gain_ref[pl.ds(first + k, 1), :]).astype(BF16)
+                (x_ref[(first + k) ^ FIRST].astype(F32) * scale * gain_ref[pl.ds(first + k, 1), :]).astype(BF16)
                 for k in (j, j + 1)
             ]
             total += jnp.dot(
@@ -66,15 +62,21 @@
         out_ref[j] = own
 
 
+def stage_kernel(own_ref, gain_ref, own_out, gain_out):
+    own_out[...] = own_ref[...]
+    gain_out[...] = gain_ref[...]
+
+
 def turn_kernel(v_ref, out_ref):
-    turned = v_ref[...].T
-    shape = (SUM_ROWS, turned.shape[1])
-    row = lax.broadcasted_iota(jnp.int32, shape, 0)
-    block = lax.broadcasted_iota(jnp.int32, shape, 1) // LANES
+    tokens = v_ref.shape[0]
+    row = lax.broadcasted_iota(jnp.int32, (SUM_ROWS, tokens), 0)
+    block = lax.broadcasted_iota(jnp.int32, (SUM_ROWS, tokens), 1) // LANES
     picks = jnp.where(row == block, 1.0, 0.0).astype(BF16)
-    for i in range(2):
-        out_ref[0, i, 0:LANES, :] = turned[i * LANES : (i + 1) * LANES]
-        out_ref[0, i, LANES : LANES + SUM_ROWS, :] = picks
+    for j in range(out_ref.shape[0]):
+        for i in range(2):
+            at = slice((2 * j + i) * LANES, (2 * j + i + 1) * LANES)
+            out_ref[j, i, 0:LANES, :] = v_ref[:, at].T
+            out_ref[j, i, LANES : LANES + SUM_ROWS, :] = picks
 
 
 def attend_kernel(
@@ -103,19 +105,19 @@
         vt_copy(g).start()
 
     def put(pair, sums, log_sum):
-        out_ref[pair, 0:half, :] = sums.astype(BF16)
+        out_ref[pair ^ FIRST, 0:half, :] = sums.astype(BF16)
         high = log_sum.astype(BF16).astype(F32)
         mid = (log_sum - high).astype(BF16).astype(F32)
         low = log_sum - high - mid
         stats = jnp.where(sub == 0, high, jnp.where(sub == 1, mid, jnp.where(sub == 2, low, 0.0)))
-        out_ref[pair, half : half + STAT_ROWS, :] = stats.astype(BF16)
+        out_ref[pair ^ FIRST, half : half + STAT_ROWS, :] = stats.astype(BF16)
 
     def rows_of(b):
         return slice(b * LANES, (b + 1) * LANES)
 
     def score(g, count, clear, s_ref, m_ref):
         none = jnp.zeros((half, LANES), BF16)
-        q0, q1 = q_ref[2 * g], q_ref[2 * g + 1]
+        q0, q1 = q_ref[(2 * g) ^ FIRST], q_ref[(2 * g + 1) ^ FIRST]
         placed = jnp.concatenate(
             [
                 jnp.concatenate([jnp.where(left, q0, none), none], axis=1),
@@ -233,7 +235,7 @@
         first = (rep_ref[0] ^ i) * each
         update = jnp.dot(attended, w_ref[...], preferred_element_type=F32)
         for j in range(each):
-            out_ref[first + j] = update[:, j * LANES : (j + 1) * LANES].astype(BF16)
+            out_ref[(first + j) ^ FIRST] = update[:, j * LANES : (j + 1) * LANES].astype(BF16)
 
 
 def sum_kernel(part_ref, out_ref):
@@ -255,7 +257,10 @@
 
 
 def swapped(blocks):
-    return lax.all_to_all(blocks, "seg", split_axis=0, concat_axis=0, tiled=True)
+    order = [[j ^ FIRST for j in range(blocks.shape[0])]]
+    return lax.all_to_all(
+        blocks, "seg", split_axis=0, concat_axis=0, tiled=True, axis_index_groups=order
+    )
 
 
 def sublayer(
@@ -283,7 +288,22 @@
 
     wq, wq_near, wq_far, wq_both = over_rep(query_weight)
     x_all = swapped(jnp.broadcast_to(decoder_rows[None], (segs, rows, own)))
-    wq, gain = pl.pallas_call(
+    groups, wide = inner // (2 * LANES), 2 * LANES
+    height = LANES + SUM_ROWS
+    steps = 4
+    turn_call = pl.pallas_call(
+        turn_kernel,
+        grid=(steps,),
+        out_shape=jax.ShapeDtypeStruct((groups, 2, height, tokens), BF16),
+        in_specs=[pl.BlockSpec((tokens, inner // steps), lambda i: (0, i))],
+        out_specs=pl.BlockSpec((groups // steps, 2, height, tokens), lambda i: (i, 0, 0, 0)),
+        compiler_params=params(51),
+        cost_estimate=cost(2 * inner * tokens * 512, 8 << 20),
+        name="turn",
+    )
+    values_t = turn_call(value_codes[0])
+
+    stage_call = pl.pallas_call(
         stage_kernel,
         out_shape=(
             jax.ShapeDtypeStruct(wq.shape, BF16),
@@ -294,7 +314,8 @@
         compiler_params=params(8),
         cost_estimate=cost(1 << 24, 1 << 20),
         name="stage",
-    )(wq, gain)
+    )
+    wq, gain = stage_call(wq, gain)
     query_call = pl.pallas_call(
         query_kernel,
         out_shape=jax.ShapeDtypeStruct((segs, head_dim, LANES), BF16),
@@ -306,19 +327,6 @@
     )
     query_sent = query_call(rep, x_all, gain, wq, wq_near, wq_far, wq_both)
     queries = swapped(query_sent)
-
-    groups, wide = inner // (2 * LANES), 2 * LANES
-    height = LANES + SUM_ROWS
-    values_t = pl.pallas_call(
-        turn_kernel,
-        grid=(groups,),
-        out_shape=jax.ShapeDtypeStruct((groups, 2, height, tokens), BF16),
-        in_specs=[pl.BlockSpec((tokens, wide), lambda i: (0, i))],
-        out_specs=pl.BlockSpec((1, 2, height, tokens), lambda i: (i, 0, 0, 0)),
-        compiler_params=params(16),
-        cost_estimate=cost(2 * inner * tokens * 512, 8 << 20),
-        name="turn",
-    )(value_codes[0])
 
     parts = pl.pallas_call(
         attend_kernel,

time: 88 us -> 83.9 us (0.953)
  starting transfers between devices: 24.6 us -> 32.4 us
  waiting for transfers between devices: 23.8 us -> 16.9 us
  local copies, waits for them, and re-layouts: 8.19 us -> 3.91 us
  blocking collectives: 18.4 us -> 14.9 us
  Pallas kernels: 11.6 us -> 14.3 us
    all_to_all x3, starting transfers between devices: 17.2 us -> 25.7 us  [swapped(): lax.all_to_all(blocks, 'seg', split_axis=0, concat_axis=0, tiled=True, ax...]
    all_to_all x3, waiting for transfers between devices: 11 us -> 4.68 us  [swapped(): lax.all_to_all(blocks, 'seg', split_axis=0, concat_axis=0, tiled=True, ax...]
    unnamed x14 -> x10, local copies, waits for them, and re-layouts: 5.97 us -> 1.68 us
    all_to_all x1, blocking collectives: 18.4 us -> 14.9 us  [swapped(): lax.all_to_all(blocks, 'seg', split_axis=0, concat_axis=0, tiled=True, ax...]
    pallas_call x2, Pallas kernels: 2.65 us -> 5.41 us  [the longest x1 5.39 us: sublayer(): values_t = turn_call(value_codes[0])]
  transfers between devices with their start and end apart: 9 -> 9, of which waited for: 4 -> 3; matrix products, arithmetic and copies ran while one was open for 3% -> 3% of each run, Pallas kernels for 3% -> 7%
where the time goes in v3:
time: 83.9 us; the launch traced here: 83.2 us
  starting transfers between devices  32.4 us (39%)
  waiting for transfers between devices  16.9 us (20%)
  blocking collectives  14.9 us (18%)
  Pallas kernels  14.3 us (17%)
  local copies, waits for them, and re-layouts  3.91 us (5%)
    all_to_all x3, starting transfers between devices, swapped(): lax.all_to_all(blocks, 'seg', split_axis=0, concat_axis=0, tiled=True, ax...  25.7 us
    all_to_all x1, blocking collectives, swapped(): lax.all_to_all(blocks, 'seg', split_axis=0, concat_axis=0, tiled=True, ax...  14.9 us
    ppermute x2, waiting for transfers between devices, over_rep(): far = lax.ppermute(block, 'rep', CHIP)  10.6 us
    pallas_call x1, Pallas kernels, sublayer(): pl.pallas_call(attend_kernel, out_shape=jax.ShapeDtypeStruct((segs, head_...  6.35 us
    ppermute x2, starting transfers between devices, over_rep(): far = lax.ppermute(block, 'rep', CHIP)  6.07 us
    pallas_call x1, Pallas kernels, sublayer(): values_t = turn_call(value_codes[0])  5.39 us
    all_to_all x3, waiting for transfers between devices, swapped(): lax.all_to_all(blocks, 'seg', split_axis=0, concat_axis=0, tiled=True, ax...  4.68 us
  transfers between devices with their start and end apart: 9, of which 3 were waited for; matrix products, arithmetic and copies ran while one was open for 3% of the time, Pallas kernels for 7%

profile of v3, /device:TPU:0, one launch (start us, length us, event | category | flops | bytes accessed | tf_op | source)
XLA Modules:
  0.0 83.2 jit_solution(2449926082902804745)
XLA Ops:
  0.0 0.0 copy-start.3
  0.0 0.0 copy-start.4
  0.0 3.3 %collective-permute-start.1 = (bf16[1024,128]{1,0:T(8,128)(2,1)}, bf16[1024,128]{1,0:T(8,128)(2,1)S(1)}, u32[]{:S(2)}, u32[]{:S(2)}) collective-permute-start(bf16[1024,128]{1,0:T(8,128)(2,1)} %own_ref.1), channel_id=1, source_target_pairs={{0,2},{1,3},{2,0},{3,1},{4,6},{5,7},{6,4},{7,5},{8,10},{9,11},{10,... | collective-permute-start | bytes 786440 | tf_op jit(solution)/shard_map/ppermute | solution.py:253
  3.3 1.6 %broadcast_in_dim.15 = bf16[32,64,128]{2,1,0:T(8,128)(2,1)} broadcast(bf16[64,128]{1,0:T(8,128)(2,1)} %param.9), dimensions={1,2} | broadcast | bytes 540672 | tf_op jit(solution)/shard_map/broadcast_in_dim | solution.py:290
  5.0 10.1 %all-to-all-start = ((bf16[32,64,128]{2,1,0:T(8,128)(2,1)}), bf16[32,64,128]{2,1,0:T(8,128)(2,1)S(1)}, u32[]{:S(2)}, u32[]{:S(2)}) async-start(bf16[32,64,128]{2,1,0:T(8,128)(2,1)} %broadcast_in_dim.15), calls=%async_computation | async-start | bytes 1048576 | tf_op jit(solution)/shard_map/all_to_all | solution.py:261
  15.1 0.1 collective-permute-start
  15.2 0.0 collective-permute-done.1.refs_2_
  15.2 0.5 collective-permute-start.2
  15.7 0.0 copy-start.1
  15.7 0.9 %copy-done.1 = bf16[1024,128]{1,0:T(8,128)(2,1)S(1)} copy-done((bf16[1024,128]{1,0:T(8,128)(2,1)S(1)}, bf16[1024,128]{1,0:T(8,128)(2,1)}, u32[]{:S(2)}) %copy-start.1) | copy-done | bytes 262168
  16.6 0.0 copy-start.2
  16.6 0.7 copy-done.2
  17.4 0.0 collective-permute-done.refs_1_
  17.4 4.7 %all-to-all-done.x_ref = bf16[32,64,128]{2,1,0:T(8,128)(2,1)S(1)} async-done(((bf16[32,64,128]{2,1,0:T(8,128)(2,1)}), bf16[32,64,128]{2,1,0:T(8,128)(2,1)S(1)}, u32[]{:S(2)}, u32[]{:S(2)}) %all-to-all-start) | async-done | bytes 524320 | tf_op jit(solution)/shard_map/all_to_all | solution.py:261
  22.1 0.0 collective-permute-done.2.refs_3_
  22.1 1.4 %query.1 = bf16[32,64,128]{2,1,0:T(8,128)(2,1)} custom-call(s32[1]{0:T(128)} %bitcast.rep_ref, bf16[32,64,128]{2,1,0:T(8,128)(2,1)S(1)} %all-to-all-done.x_ref, f32[32,128]{1,0:T(8,128)S(1)} %get-tuple-element.7.gain_ref, bf16[1024,128]{1,0:T(8,128)(2,1)S(1)} %get-tuple-element.8.refs_0_, bf16[1024,128]{1,0:T(8,128)(2,1)S(1)} %collective-permute-done.refs_1_, ...), custom_call_target="tpu_custom_call" | custom-call | flops 67108864 | bytes 2097152 | tf_op jit(solution)/shard_map/query/pallas_call | solution.py:328
  23.4 8.2 %all-to-all-start.1 = ((bf16[32,64,128]{2,1,0:T(8,128)(2,1)}), bf16[32,64,128]{2,1,0:T(8,128)(2,1)S(1)}, u32[]{:S(2)}, u32[]{:S(2)}) async-start(bf16[32,64,128]{2,1,0:T(8,128)(2,1)} %query.1), calls=%async_computation.1 | async-start | bytes 1048576 | tf_op jit(solution)/shard_map/all_to_all | solution.py:261
  31.6 0.0 copy-done.3
  31.7 0.1 broadcast_in_dim.17
  31.8 0.1 reshape.26.lvs_ref
  31.9 0.1 broadcast_in_dim.18
  32.0 0.1 reshape.27.ivs_ref
  32.7 0.0 copy-done.4
  32.8 0.1 broadcast_in_dim.16
  32.9 0.1 reshape.25.ks_ref
  33.0 5.4 %turn.1.vt_hbm = bf16[16,2,144,512]{3,2,1,0:T(8,128)(2,1)} custom-call(bf16[512,4096]{1,0:T(8,128)(2,1)} %bitcast.13), custom_call_target="tpu_custom_call" | custom-call | flops 2147483648 | bytes 8388608 | tf_op jit(solution)/shard_map/turn/pallas_call | solution.py:304
  38.4 0.0 all-to-all-done.1.q_ref
  38.4 0.0 copy-start
  38.4 6.3 %attend.1 = bf16[32,72,128]{2,1,0:T(8,128)(2,1)} custom-call(s32[1]{0:T(128)S(6)} %min.6.used_ref, bf16[32,64,128]{2,1,0:T(8,128)(2,1)S(1)} %all-to-all-done.1.q_ref, f32[4,4096]{1,0:T(4,128)S(1)} %reshape.25.ks_ref, f32[4,4096]{1,0:T(4,128)S(1)} %reshape.26.lvs_ref, f32[4,4096]{1,0:T(4,128)S(1)} %reshape.27.ivs_ref, bf16[512,4096]{1,0:T(8,128)(2,1)} %bitcast.12, ...), custom_call_target="tpu_custom_call" | custom-call | flops 2147483648 | bytes 9437184 | tf_op jit(solution)/shard_map/attend/pallas_call | solution.py:331
  44.7 7.4 %all-to-all-start.2 = ((bf16[32,72,128]{2,1,0:T(8,128)(2,1)}), bf16[32,72,128]{2,1,0:T(8,128)(2,1)S(1)}, u32[]{:S(2)}, u32[]{:S(2)}) async-start(bf16[32,72,128]{2,1,0:T(8,128)(2,1)} %attend.1), calls=%async_computation.2 | async-start | bytes 1179648 | tf_op jit(solution)/shard_map/all_to_all | solution.py:261
  52.1 0.0 copy-done
  52.1 2.8 %collective-permute-start.4 = (bf16[128,1024]{1,0:T(8,128)(2,1)S(1)}, bf16[128,1024]{1,0:T(8,128)(2,1)S(1)}, u32[]{:S(2)}, u32[]{:S(2)}) collective-permute-start(bf16[128,1024]{1,0:T(8,128)(2,1)S(1)} %copy-done), channel_id=1, source_target_pairs={{0,2},{1,3},{2,0},{3,1},{4,6},{5,7},{6,4},{7,5},{8,10},{9,11},{10,... | collective-permute-start | bytes 786440 | tf_op jit(solution)/shard_map/ppermute | solution.py:253
  54.9 0.0 collective-permute-start.3
  54.9 10.6 %collective-permute-done.4.refs_2_ = bf16[128,1024]{1,0:T(8,128)(2,1)S(1)} collective-permute-done((bf16[128,1024]{1,0:T(8,128)(2,1)S(1)}, bf16[128,1024]{1,0:T(8,128)(2,1)S(1)}, u32[]{:S(2)}, u32[]{:S(2)}) %collective-permute-start.4) | collective-permute-done | bytes 262176 | tf_op jit(solution)/shard_map/ppermute | solution.py:253
  65.5 0.0 collective-permute-start.5
  65.5 0.0 collective-permute-done.3.refs_1_
  65.5 1.5 %collective-permute-done.5.refs_3_ = bf16[128,1024]{1,0:T(8,128)(2,1)S(1)} collective-permute-done((bf16[128,1024]{1,0:T(8,128)(2,1)S(1)}, bf16[128,1024]{1,0:T(8,128)(2,1)S(1)}, u32[]{:S(2)}, u32[]{:S(2)}) %collective-permute-start.5) | collective-permute-done | bytes 262176 | tf_op jit(solution)/shard_map/ppermute | solution.py:255
  67.1 0.0 all-to-all-done.2.part_ref
  67.1 0.5 output.1
  67.6 14.9 %all_to_all.20.part_ref = bf16[32,64,128]{2,1,0:T(8,128)(2,1)S(1)} all-to-all(bf16[32,64,128]{2,1,0:T(8,128)(2,1)S(1)} %output.1), channel_id=1, replica_groups={{40,44,32,36,56,60,48,52,8,12,0,4,24,28,16,20,104,108,96,100,120,124,11..., dimensions={0} | all-to-all | bytes 1048576 | tf_op jit(solution)/shard_map/all_to_all | solution.py:261
  82.5 0.7 gather_sum.1
  (3 shorter events, 0.0 us)
Async XLA Ops:
  0.0 31.6 %copy-start.3 = (f32[1,4,64]{2,1,0:T(4,128)S(1)}, f32[1,4,64]{2,1,0:T(4,128)}, u32[]{:S(2)}) copy-start(f32[1,4,64]{2,1,0:T(4,128)} %param.15) | copy-start | bytes 3076
  0.0 32.7 %copy-start.4 = (f32[1,4,64]{2,1,0:T(4,128)S(1)}, f32[1,4,64]{2,1,0:T(4,128)}, u32[]{:S(2)}) copy-start(f32[1,4,64]{2,1,0:T(4,128)} %param.13) | copy-start | bytes 3076
  0.0 15.2 %collective-permute-start.1 = (bf16[1024,128]{1,0:T(8,128)(2,1)}, bf16[1024,128]{1,0:T(8,128)(2,1)S(1)}, u32[]{:S(2)}, u32[]{:S(2)}) collective-permute-start(bf16[1024,128]{1,0:T(8,128)(2,1)} %own_ref.1), channel_id=1, source_target_pairs={{0,2},{1,3},{2,0},{3,1},{4,6},{5,7},{6,4},{7,5},{8,10},{9,11},{10,... | collective-permute-start | bytes 786440 | tf_op jit(solution)/shard_map/ppermute | solution.py:253
  5.0 17.1 %all-to-all-start = ((bf16[32,64,128]{2,1,0:T(8,128)(2,1)}), bf16[32,64,128]{2,1,0:T(8,128)(2,1)S(1)}, u32[]{:S(2)}, u32[]{:S(2)}) async-start(bf16[32,64,128]{2,1,0:T(8,128)(2,1)} %broadcast_in_dim.15), calls=%async_computation | async-start | bytes 1048576 | tf_op jit(solution)/shard_map/all_to_all | solution.py:261
  15.1 2.3 %collective-permute-start = (bf16[1024,128]{1,0:T(8,128)(2,1)}, bf16[1024,128]{1,0:T(8,128)(2,1)S(1)}, u32[]{:S(2)}, u32[]{:S(2)}) collective-permute-start(bf16[1024,128]{1,0:T(8,128)(2,1)} %own_ref.1), channel_id=1, source_target_pairs={{0,1},{1,0},{2,3},{3,2},{4,5},{5,4},{6,7},{7,6},{8,9},{9,8},{10,11... | collective-permute-start | bytes 786440 | tf_op jit(solution)/shard_map/ppermute | solution.py:254
  15.2 6.9 %collective-permute-start.2 = (bf16[1024,128]{1,0:T(8,128)(2,1)S(1)}, bf16[1024,128]{1,0:T(8,128)(2,1)S(1)}, u32[]{:S(2)}, u32[]{:S(2)}) collective-permute-start(bf16[1024,128]{1,0:T(8,128)(2,1)S(1)} %collective-permute-done.1.refs_2_), channel_id=1, source_target_pairs={{0,1},{1,0},{2,3},{3,2},{4,5},{5,4},{6,7},{7,6},{8,9},{9,8},{10,11... | collective-permute-start | bytes 786440 | tf_op jit(solution)/shard_map/ppermute | solution.py:255
  15.7 0.9 %copy-start.1 = (bf16[1024,128]{1,0:T(8,128)(2,1)S(1)}, bf16[1024,128]{1,0:T(8,128)(2,1)}, u32[]{:S(2)}) copy-start(bf16[1024,128]{1,0:T(8,128)(2,1)} %own_ref.1) | copy-start | bytes 786436
  16.6 0.7 copy-start.2
  23.4 14.9 %all-to-all-start.1 = ((bf16[32,64,128]{2,1,0:T(8,128)(2,1)}), bf16[32,64,128]{2,1,0:T(8,128)(2,1)S(1)}, u32[]{:S(2)}, u32[]{:S(2)}) async-start(bf16[32,64,128]{2,1,0:T(8,128)(2,1)} %query.1), calls=%async_computation.1 | async-start | bytes 1048576 | tf_op jit(solution)/shard_map/all_to_all | solution.py:261
  38.4 13.8 %copy-start = (bf16[128,1024]{1,0:T(8,128)(2,1)S(1)}, bf16[128,1024]{1,0:T(8,128)(2,1)}, u32[]{:S(2)}) copy-start(bf16[128,1024]{1,0:T(8,128)(2,1)} %refs_0_.1) | copy-start | bytes 786436
  44.7 22.3 %all-to-all-start.2 = ((bf16[32,72,128]{2,1,0:T(8,128)(2,1)}), bf16[32,72,128]{2,1,0:T(8,128)(2,1)S(1)}, u32[]{:S(2)}, u32[]{:S(2)}) async-start(bf16[32,72,128]{2,1,0:T(8,128)(2,1)} %attend.1), calls=%async_computation.2 | async-start | bytes 1179648 | tf_op jit(solution)/shard_map/all_to_all | solution.py:261
  52.1 13.4 %collective-permute-start.4 = (bf16[128,1024]{1,0:T(8,128)(2,1)S(1)}, bf16[128,1024]{1,0:T(8,128)(2,1)S(1)}, u32[]{:S(2)}, u32[]{:S(2)}) collective-permute-start(bf16[128,1024]{1,0:T(8,128)(2,1)S(1)} %copy-done), channel_id=1, source_target_pairs={{0,2},{1,3},{2,0},{3,1},{4,6},{5,7},{6,4},{7,5},{8,10},{9,11},{10,... | collective-permute-start | bytes 786440 | tf_op jit(solution)/shard_map/ppermute | solution.py:253
  54.9 10.7 %collective-permute-start.3 = (bf16[128,1024]{1,0:T(8,128)(2,1)S(1)}, bf16[128,1024]{1,0:T(8,128)(2,1)S(1)}, u32[]{:S(2)}, u32[]{:S(2)}) collective-permute-start(bf16[128,1024]{1,0:T(8,128)(2,1)S(1)} %copy-done), channel_id=1, source_target_pairs={{0,1},{1,0},{2,3},{3,2},{4,5},{5,4},{6,7},{7,6},{8,9},{9,8},{10,11... | collective-permute-start | bytes 786440 | tf_op jit(solution)/shard_map/ppermute | solution.py:254
  65.5 1.5 %collective-permute-start.5 = (bf16[128,1024]{1,0:T(8,128)(2,1)S(1)}, bf16[128,1024]{1,0:T(8,128)(2,1)S(1)}, u32[]{:S(2)}, u32[]{:S(2)}) collective-permute-start(bf16[128,1024]{1,0:T(8,128)(2,1)S(1)} %collective-permute-done.4.refs_2_), channel_id=1, source_target_pairs={{0,1},{1,0},{2,3},{3,2},{4,5},{5,4},{6,7},{7,6},{8,9},{9,8},{10,11... | collective-permute-start | bytes 786440 | tf_op jit(solution)/shard_map/ppermute | solution.py:255
